TPU v7x, 512 devices: a whole 4x4x16 slice. The times are simulated.
512 devices in a mesh: gx: 32 (over x, y, core), gy: 16 (over z).
Axes of the slice: x: 4, y: 4, z: 16, core: 2. Of those that a mesh axis runs over, the one named last changes fastest.
Arguments:
- node_disp: float32 [2, 1024, 4096], P(None, 'gx', 'gy'), may hold values from -0.24 to 0.24
- node_vel: float32 [2, 1024, 4096], P(None, 'gx', 'gy'), may hold values from -6 to 6
- node_mass: float32 [1024, 4096], P('gx', 'gy'), may hold values from 0.5 to 2
- zone_mass: float32 [1024, 4096], P('gx', 'gy'), may hold values from 0.5 to 2
- zone_energy: float32 [1024, 4096], P('gx', 'gy'), may hold values from 0.3 to 7.5
- master_block: bfloat16 [512, 4, 16384], P(('gx', 'gy')), may hold values from -3 to 3, as said below
- owner: int32 [1], replicated, may hold values from 0 to 511
- pair_node: int32 [512, 1024], P(('gx', 'gy')), may hold values from 0 to 8191
- pair_segment: int32 [512, 1024], P(('gx', 'gy')), may hold values from 0 to 16382
- pair_side: int32 [512, 1024], P(('gx', 'gy')), may hold values 0 or 1
- pair_count: int32 [512], P(('gx', 'gy')), may hold values from 0 to 1024, as said below
Outputs:
- new_vel: float32 [2, 1024, 4096], P(None, 'gx', 'gy')
- new_disp: float32 [2, 1024, 4096], P(None, 'gx', 'gy')
- master_impulse: float32 [3, 16384], P(None, ('gx', 'gy'))
Inputs may be any that keep to these rules, and one draw needn't show every extreme that they name: `pair_node`: local node numbers, row-major over a device's 32 x 256 block. `pair_count`: at most 1024; one device has exactly 1024 in every draw; slots at or past a device's count are not pairs. `master_block`: rows 0 and 1 lie within -0.25 to 0.25.
All inputs are finite; a program needn't handle non-finite values. No bound on the sum of `pair_side` on one device may be relied on, other than what follows from the above.
Results may differ from a plain program's by a relative error of at most 0.0015.
Values may be sent and summed in bfloat16 or wider, within the bound.
No kernel may reach another device: no remote copies, remote signals or barrier semaphores. Data moves between devices by JAX's collectives and lax.ppermute only.
A program may use at most 128 MiB of HBM per device.

v0:
```python
import jax
import jax.numpy as jnp
from jax import lax
from jax.sharding import Mesh
from jax.sharding import PartitionSpec as P

GX = ("gx_0", "gx_1", "gx_2")
GX_GY = ("gx_0", "gx_1", "gx_2", "gy")


STIFFNESS = 10.0
GAP_SCALE = 0.05


def broadcast_by_axis(value, axes, root):
    value = jnp.where(lax.axis_index(axes) == root, value, jnp.zeros_like(value))
    for axis in axes:
        value = lax.psum(value, axis)
    return value


def with_halo(cells, sides, width):
    for axis, dim in sides:
        count = lax.axis_size(axis)
        ends = count - 1
        head = lax.slice_in_dim(cells, 0, width, axis=dim)
        tail = lax.slice_in_dim(cells, cells.shape[dim] - width, cells.shape[dim], axis=dim)
        cells = jnp.concatenate(
            [
                lax.ppermute(tail, axis, [(i, (i + 1) % count) for i in range(ends)]),
                cells,
                lax.ppermute(head, axis, [((i + 1) % count, i) for i in range(ends)]),
            ],
            axis=dim,
        )
    return cells


def over_axes(value, axes):
    for axis in axes:
        value = lax.pmin(value, axis)
    return value


def own_block(tiles, axes, turns):
    dims = [lax.axis_size(a) for a in axes]
    tiles = tiles.reshape(*dims, *tiles.shape[1:])
    tiles = tiles.transpose(*turns, *range(len(axes), tiles.ndim))
    tiles = tiles.reshape(-1, *tiles.shape[len(axes) :])
    for k in turns:
        tiles = lax.psum_scatter(tiles, axes[k], scatter_dimension=0, tiled=True)
    return tiles[0]


def cut_along(value, dim, length):
    dims = value.shape
    tiles = value.reshape(*dims[:dim], length, dims[dim] // length, *dims[dim + 1 :])
    return jnp.moveaxis(tiles, dim, 0)


def scatter_axes(value, axes, turns, dim):
    length = lax.axis_size(axes)
    return own_block(cut_along(value, dim, length), axes, turns)


def corner_forces(corner_a, corner_b, corner_c, corner_e, zone_load, zone_live):
    first_dx = 1.0 + corner_c[0] - corner_a[0]
    first_dy = 1.0 + corner_c[1] - corner_a[1]
    second_dx = -1.0 + corner_e[0] - corner_b[0]
    second_dy = 1.0 + corner_e[1] - corner_b[1]
    zone_area = 0.5 * (first_dx * second_dy - second_dx * first_dy)
    safe_area = jnp.where(zone_live, zone_area, 1.0)
    half_press = jnp.where(zone_live, 0.2 * zone_load / safe_area, 0.0)
    force_a = jnp.stack([-half_press * second_dy, half_press * second_dx])
    force_b = jnp.stack([half_press * first_dy, -half_press * first_dx])
    return (safe_area, force_a, force_b, -force_a, -force_b)


def contact_terms(slave_disp, seg_start, seg_end, side_flags, live_mask):
    rel_x = slave_disp[0] - seg_start[0] + 0.5
    rel_y = slave_disp[1] - seg_start[1]
    along_x = 1.0 + seg_end[0] - seg_start[0]
    along_y = seg_end[1] - seg_start[1]
    along_sq = along_x * along_x + along_y * along_y
    length = jnp.sqrt(along_sq)
    fraction = (rel_x * along_x + rel_y * along_y) / along_sq
    normal_x = -along_y / length
    normal_y = along_x / length
    gap_size = normal_x * rel_x + normal_y * rel_y
    side_sign = 1.0 - 2.0 * side_flags.astype(jnp.float32)
    magnitude = jnp.where(
        live_mask, STIFFNESS * GAP_SCALE * jax.nn.softplus(-side_sign * gap_size / GAP_SCALE), 0.0
    )
    slave_push = jnp.stack([magnitude * side_sign * normal_x, magnitude * side_sign * normal_y])
    react_first = jnp.stack(
        [
            -(1.0 - fraction) * slave_push[0],
            -(1.0 - fraction) * slave_push[1],
            (1.0 - fraction) * magnitude,
        ]
    )
    react_second = jnp.stack(
        [-fraction * slave_push[0], -fraction * slave_push[1], fraction * magnitude]
    )
    return (slave_push, react_first, react_second)


def shards(
    node_disp,
    node_vel,
    node_mass,
    zone_mass,
    zone_energy,
    master_block,
    owner,
    pair_node,
    pair_segment,
    pair_side,
    pair_count,
):
    row_count = node_disp.shape[1]
    col_count = node_disp.shape[2]
    row_base = lax.axis_index(GX) * row_count
    col_base = lax.axis_index("gy") * col_count
    total_rows = row_count * lax.axis_size(GX)
    total_cols = col_count * lax.axis_size("gy")
    surface = broadcast_by_axis(master_block[0], GX_GY, owner[0])
    packed = jnp.concatenate([node_disp, (zone_energy * zone_mass)[None]], axis=0)
    extended = with_halo(packed.astype(jnp.bfloat16), ((GX, 1), ("gy", 2)), 1).astype(packed.dtype)
    zone_rows = row_base - 1 + jnp.arange(row_count + 1, dtype=jnp.int32)
    zone_cols = col_base - 1 + jnp.arange(col_count + 1, dtype=jnp.int32)
    zone_live = (
        (zone_rows[:, None] >= 0)
        & (zone_rows[:, None] < total_rows - 1)
        & (zone_cols[None, :] >= 0)
        & (zone_cols[None, :] < total_cols - 1)
    )
    safe_area, force_a, force_b, force_c, force_e = corner_forces(
        extended[:2, : row_count + 1, : col_count + 1],
        extended[:2, 1:, : col_count + 1],
        extended[:2, 1:, 1:],
        extended[:2, : row_count + 1, 1:],
        extended[2, : row_count + 1, : col_count + 1],
        zone_live,
    )
    node_force = (
        force_a[:, 1:, 1:]
        + force_b[:, :row_count, 1:]
        + force_c[:, :row_count, :col_count]
        + force_e[:, 1:, :col_count]
    )
    own_area = safe_area[1:, 1:]
    own_live = zone_live[1:, 1:]
    zone_ratio = jnp.where(own_live, jnp.sqrt(own_area) / jnp.sqrt(0.56 * zone_energy), 1e30)
    step_size = 0.3 * over_axes(jnp.min(zone_ratio), GX_GY)
    coords = surface[0:2].astype(jnp.float32)
    flat_disp = node_disp.reshape(2, row_count * col_count)
    live_count = pair_count[0]
    block_count = (live_count + 127) // 128
    surface_nodes = surface.shape[1]

    def contact_block(block_index, loop_state):
        pushed, reaction = loop_state
        first_pair = block_index * 128
        slave_nodes = lax.dynamic_slice_in_dim(pair_node[0], first_pair, 128)
        segment_ids = lax.dynamic_slice_in_dim(pair_segment[0], first_pair, 128)
        side_flags = lax.dynamic_slice_in_dim(pair_side[0], first_pair, 128)
        live_mask = first_pair + jnp.arange(128, dtype=jnp.int32) < live_count
        slave_disp = jnp.take(flat_disp, slave_nodes, axis=1)
        seg_start = jnp.take(coords, segment_ids, axis=1)
        seg_end = jnp.take(coords, segment_ids + 1, axis=1)
        slave_push, react_first, react_second = contact_terms(
            slave_disp, seg_start, seg_end, side_flags, live_mask
        )
        pushed = pushed.at[:, slave_nodes].add(slave_push)
        reaction = (
            reaction.at[:, segment_ids].add(react_first).at[:, segment_ids + 1].add(react_second)
        )
        return (pushed, reaction)

    pushed, reaction = lax.fori_loop(
        0,
        block_count,
        contact_block,
        (
            jnp.zeros((2, row_count * col_count), jnp.float32),
            jnp.zeros((3, surface_nodes), jnp.float32),
        ),
    )
    total_force = node_force + pushed.reshape(2, row_count, col_count)
    new_vel = node_vel + step_size * total_force / node_mass
    new_disp = node_disp + step_size * new_vel
    share_width = surface_nodes // (lax.axis_size(GX) * lax.axis_size("gy"))
    my_index = lax.axis_index(GX) * lax.axis_size("gy") + lax.axis_index("gy")
    reaction_share = scatter_axes(reaction, GX_GY, (2, 0, 1, 3), 1)
    prior_impulse = lax.dynamic_slice_in_dim(
        surface[2:4], my_index * share_width, share_width, 1
    ).astype(jnp.float32)
    master_impulse = jnp.concatenate(
        [prior_impulse + step_size * reaction_share[0:2], step_size * reaction_share[2:3]], axis=0
    )
    return (new_vel, new_disp, master_impulse)


def solution(mesh):
    split = Mesh(mesh.devices.reshape(4, 4, 2, mesh.shape["gy"]), ("gx_0", "gx_1", "gx_2", "gy"))
    in_specs = (
        P(None, GX, "gy"),
        P(None, GX, "gy"),
        P(GX, "gy"),
        P(GX, "gy"),
        P(GX, "gy"),
        P(GX_GY, None, None),
        P(),
        P(GX_GY, None),
        P(GX_GY, None),
        P(GX_GY, None),
        P(GX_GY),
    )
    out_specs = (P(None, GX, "gy"), P(None, GX, "gy"), P(None, GX_GY))
    return jax.shard_map(
        shards, mesh=split, in_specs=in_specs, out_specs=out_specs, check_vma=False
    )
```

profile of v0, /device:TPU:4, one launch (start us, length us, event | category | flops | bytes accessed | tf_op | source)
XLA Modules:
  0.0 805.6 jit_solution(4773205051423857249)
XLA Ops:
  7.9 0.7 select_bitcast_fusion.3
  8.7 0.8 convert.7
  9.5 0.8 fusion.25
  10.3 1.9 collective-permute-start
  12.2 5.8 collective-permute-start.1
  18.0 52.7 %all-reduce.11.cloned.1.call-done = bf16[4,16384]{1,0:T(4,128)(2,1)} async-done(((bf16[4,16384]{1,0:T(4,128)(2,1)}), bf16[4,16384]{1,0:T(4,128)(2,1)}) %all-reduce.11.cloned.1.call-update) | async-done | bytes 131088 | tf_op jit(solution)/shard_map/psum | solution.py:18
  70.8 0.1 and_and_fusion
  71.5 3.3 copy.80
  74.9 1.3 dynamic-slice.12
  76.2 1.3 dynamic-slice.14
  77.4 1.3 dynamic-slice.16
  78.7 1.3 dynamic-slice.18
  80.0 51.2 %all-reduce.13.cloned.1.call-done = bf16[4,16384]{1,0:T(4,128)(2,1)} async-done(((bf16[4,16384]{1,0:T(4,128)(2,1)}), bf16[4,16384]{1,0:T(4,128)(2,1)}) %all-reduce.13.cloned.1.call-update) | async-done | bytes 131088 | tf_op jit(solution)/shard_map/psum | solution.py:18
  131.3 0.1 fusion.33
  131.4 3.4 collective-permute-start.2
  134.8 1.3 collective-permute-start.3
  136.1 0.2 collective-permute-done.2
  136.4 4.2 collective-permute-done.3
  140.6 0.1 maximum_convert_fusion
  140.7 32.9 %all-reduce.15.cloned.1.call-done = bf16[4,16384]{1,0:T(4,128)(2,1)} async-done(((bf16[4,16384]{1,0:T(4,128)(2,1)}), bf16[4,16384]{1,0:T(4,128)(2,1)}) %all-reduce.15.cloned.1.call-update) | async-done | bytes 131088 | tf_op jit(solution)/shard_map/psum | solution.py:18
  173.7 0.1 fusion.26
  173.9 1.5 fusion.24
  175.9 8.9 %pmin.28 = f32[]{:T(128)} all-reduce(f32[]{:T(128)} %fusion.24), channel_id=1, replica_groups=mesh['gx_0'=4,'gx_1'=4,'gx_2'=2,'gy'=16] {'gx_0'}, use_global_device_ids=true, to_apply=%region_1.2 | all-reduce | flops 1 | bytes 8 | tf_op jit(solution)/shard_map/pmin | solution.py:41
  185.5 11.1 %pmin.29 = f32[]{:T(128)} all-reduce(f32[]{:T(128)} %pmin.28), channel_id=1, replica_groups=mesh['gx_0'=4,'gx_1'=4,'gx_2'=2,'gy'=16] {'gx_1'}, use_global_device_ids=true, to_apply=%region_2.3 | all-reduce | flops 1 | bytes 8 | tf_op jit(solution)/shard_map/pmin | solution.py:41
  197.2 3.1 pmin.30
  200.3 31.9 %pmin.31 = f32[]{:T(128)} all-reduce(f32[]{:T(128)} %pmin.30), channel_id=1, replica_groups=mesh['gx_0'=4,'gx_1'=4,'gx_2'=2,'gy'=16] {'gy'}, use_global_device_ids=true, to_apply=%region_4.5 | all-reduce | flops 1 | bytes 8 | tf_op jit(solution)/shard_map/pmin | solution.py:41
  232.8 80.7 %all-reduce.17.cloned.1.call-done = bf16[4,16384]{1,0:T(4,128)(2,1)} async-done(((bf16[4,16384]{1,0:T(4,128)(2,1)}), bf16[4,16384]{1,0:T(4,128)(2,1)}) %all-reduce.17.cloned.1.call-update) | async-done | bytes 131088 | tf_op jit(solution)/shard_map/psum | solution.py:18
  313.5 1.1 fusion.32
  314.6 5.0 copy.81
  319.6 3.5 broadcast_in_dim.61
  323.1 2.2 broadcast_in_dim.60
  325.3 36.3 %while.14 = (s32[]{:T(128)}, f32[2,8192]{0,1:T(8,128)}, f32[3,16384]{0,1:T(8,128)}, s32[]{:T(128)}, s32[1,1024]{1,0:T(1,128)}, /*index=5*/s32[]{:T(128)}, s32[1,...) while((s32[]{:T(128)}, f32[2,8192]{0,1:T(8,128)}, ...), condition=%wide.region_13.15_spmd, body=%wide.region_9.14_spmd.sunk | while | flops 17542 | bytes 83919 | solution.py:181
  325.3 0.7 fusion.36
  326.0 0.7 fusion.37
  326.6 2.8 gather_fusion.2
  329.5 0.1 copy.97
  329.5 0.7 compare_and_fusion.5
  330.2 4.0 gather_fusion
  334.3 0.1 copy.95
  334.4 4.0 gather_fusion.1
  338.4 0.1 copy.96
  338.4 1.4 negate_multiply_fusion.9
  339.8 0.7 negate_multiply_fusion.10
  340.5 0.1 copy.99
  340.6 7.7 scatter_fusion.1
  348.4 0.1 copy.100
  348.5 7.7 scatter_fusion.2
  356.2 0.1 copy.98
  356.3 5.3 scatter_fusion
  361.6 6.1 copy.84
  367.7 1.6 copy.85
  369.3 0.0 all-reduce.21.cloned.1.call-start
  369.4 0.1 negate_multiply_fusion.5
  369.5 2.8 copy.86
  372.3 287.6 %all-reduce.19.cloned.1.call-done = f32[512,3,32]{2,1,0:T(4,128)} async-done(((f32[512,3,32]{2,1,0:T(4,128)}), f32[512,3,32]{2,1,0:T(4,128)}) %all-reduce.19.cloned.1.call-update) | async-done | bytes 196624
  660.0 1.9 constant_dynamic-slice_fusion.6
  662.0 0.8 multiply_add_fusion.1
  662.7 58.5 %all-reduce.21.cloned.1.call-done = f32[256,3,32]{2,1,0:T(4,128)} async-done(((f32[256,3,32]{2,1,0:T(4,128)}), f32[256,3,32]{2,1,0:T(4,128)}) %all-reduce.21.cloned.1.call-update) | async-done | bytes 98320
  721.2 0.9 constant_dynamic-slice_fusion.5
  722.2 18.3 %all-reduce.2 = f32[64,3,32]{2,1,0:T(4,128)S(1)} all-reduce(f32[64,3,32]{2,1,0:T(4,128)S(1)} %constant_dynamic-slice_fusion.5), channel_id=4, replica_groups=mesh['gx_0'=4,'gx_1'=4,'gx_2'=2,'gy'=16] {'gx_1'}, use_global_device_ids=true, to_apply=%region_16.18.clone | all-reduce | flops 6144 | bytes 49152
  740.5 56.9 %all-reduce.3 = f32[16,3,32]{2,1,0:T(4,128)S(1)} all-reduce(f32[16,3,32]{2,1,0:T(4,128)S(1)} %constant_dynamic-slice_fusion.4), channel_id=5, replica_groups=mesh['gx_0'=4,'gx_1'=4,'gx_2'=2,'gy'=16] {'gy'}, use_global_device_ids=true, to_apply=%region_17.19.clone | all-reduce | flops 1536 | bytes 12288
  797.4 0.6 constant_dynamic-slice_fusion.3
  798.1 0.1 bitcast_add_fusion.3
  798.2 0.6 pad_maximum_fusion.5
  (36 shorter events, 0.5 us)
Async XLA Ops:
  7.2 63.5 %all-reduce.11.cloned.1.call-start = ((), (), s32[]{:S(2)}) async-start(), calls=%async_computation | async-start | bytes 262144 | tf_op jit(solution)/shard_map/psum | solution.py:18
  8.6 122.6 %all-reduce.13.cloned.1.call-start = ((), (), s32[]{:S(2)}) async-start(), calls=%async_computation.1 | async-start | bytes 262144 | tf_op jit(solution)/shard_map/psum | solution.py:18
  10.3 69.7 %collective-permute-start = (bf16[3,1,256]{2,1,0:T(2,128)(2,1)S(1)}, bf16[3,1,256]{2,1,0:T(2,128)(2,1)S(1)}, u32[]{:S(2)}, u32[]{:S(2)}) collective-permute-start(bf16[3,1,256]{2,1,0:T(2,128)(2,1)S(1)} %get-tuple-element.236), channel_id=1, source_target_pairs={{0,16},{16,32},{32,48},{48,64},{64,80},{80,96},{96,112},{112,128},... | collective-permute-start | bytes 4616 | tf_op jit(solution)/shard_map/ppermute | solution.py:30
  12.2 67.7 %collective-permute-start.1 = (bf16[3,1,256]{2,1,0:T(2,128)(2,1)S(1)}, bf16[3,1,256]{2,1,0:T(2,128)(2,1)S(1)}, u32[]{:S(2)}, u32[]{:S(2)}) collective-permute-start(bf16[3,1,256]{2,1,0:T(2,128)(2,1)S(1)} %get-tuple-element.237), channel_id=1, source_target_pairs={{16,0},{32,16},{48,32},{64,48},{80,64},{96,80},{112,96},{128,112},... | collective-permute-start | bytes 4616 | tf_op jit(solution)/shard_map/ppermute | solution.py:32
  70.7 102.9 %all-reduce.15.cloned.1.call-start = ((), (), s32[]{:S(2)}) async-start(), calls=%async_computation.2 | async-start | bytes 262144 | tf_op jit(solution)/shard_map/psum | solution.py:18
  131.2 182.3 %all-reduce.17.cloned.1.call-start = ((), (), s32[]{:S(2)}) async-start(), calls=%async_computation.3 | async-start | bytes 262144 | tf_op jit(solution)/shard_map/psum | solution.py:18
  131.4 5.0 collective-permute-start.2
  134.8 5.8 collective-permute-start.3
  173.7 486.3 %all-reduce.19.cloned.1.call-start = ((), (), s32[]{:S(2)}) async-start(), calls=%async_computation.4 | async-start | bytes 2097152
  361.6 300.3 %copy-start = (f32[2,32,256]{2,1,0:T(8,128)S(1)}, f32[2,32,256]{2,1,0:T(8,128)}, u32[]{:S(2)}) copy-start(f32[2,32,256]{2,1,0:T(8,128)} %param.15) | copy-start | bytes 196612
  361.6 300.3 %copy-start.1 = (f32[2,32,256]{2,1,0:T(8,128)S(1)}, f32[2,32,256]{2,1,0:T(8,128)}, u32[]{:S(2)}) copy-start(f32[2,32,256]{2,1,0:T(8,128)} %param.16) | copy-start | bytes 196612
  361.6 300.3 %copy-start.2 = (f32[32,256]{1,0:T(8,128)S(1)}, f32[32,256]{1,0:T(8,128)}, u32[]{:S(2)}) copy-start(f32[32,256]{1,0:T(8,128)} %param.17) | copy-start | bytes 98308
  369.3 351.9 %all-reduce.21.cloned.1.call-start = ((), (), s32[]{:S(2)}) async-start(), calls=%async_computation.5 | async-start | bytes 1048576
Sparse Core Ops, SparseCore 0:
  10.3 60.3 all-reduce.10
  73.0 58.1 all-reduce.12
  134.1 39.5 all-reduce.14
  175.8 137.7 all-reduce.16
  369.4 290.4 all-reduce.18
  662.2 59.0 all-reduce.20
where the time goes:
time: 806 us
  waiting for transfers between devices  568 us (70%)
  blocking collectives  130 us (16%)
  local copies, waits for them, and re-layouts  44.6 us (6%)
  other arithmetic  31.7 us (4%)
  between operations  18.1 us (2%)
  starting transfers between devices  12.7 us (2%)
    unnamed x8, waiting for transfers between devices  346 us
    psum x4, waiting for transfers between devices, broadcast_by_axis(): value = lax.psum(value, axis)  217 us
    unnamed x2, blocking collectives  75.2 us
    pmin x4, blocking collectives, over_axes(): value = lax.pmin(value, axis)  55.1 us
  transfers between devices with their start and end apart: 10, of which 8 were waited for; matrix products, arithmetic and copies ran while one was open for 2% of the time, Pallas kernels for 0%

commit v1 on v0

v1 whole, which is shorter than its diff:
```python
import jax
import jax.numpy as jnp
from jax import lax
from jax.experimental import pallas as pl
from jax.experimental.pallas import tpu as pltpu
from jax.sharding import Mesh
from jax.sharding import PartitionSpec as P

GX = ("gx_0", "gx_1", "gx_2")
GX_GY = ("gx_0", "gx_1", "gx_2", "gy")
NGX = 32
NGY = 16
ROWS = 32
COLS = 256
PAIRS = 1024
TOTAL_ROWS = NGX * ROWS
TOTAL_COLS = NGY * COLS
STIFFNESS = 10.0
GAP_SCALE = 0.05
BLOCK = 256

f32 = jnp.float32
bf16 = jnp.bfloat16
VMEM = pl.BlockSpec(memory_space=pltpu.VMEM)
SMEM = pl.BlockSpec(memory_space=pltpu.SMEM)


def place(ids):
    return ids[0], lax.axis_index(GX), lax.axis_index("gy")


def iota(shape, dim):
    return lax.broadcasted_iota(jnp.int32, shape, dim)


def rows_of(pieces):
    row = iota((8, 128), 0)
    tile = jnp.zeros((8, 128), f32)
    for k, piece in enumerate(pieces):
        tile = jnp.where(row == k, piece, tile)
    return tile


def column_row(columns):
    line, lane = iota((ROWS, 128), 0), iota((ROWS, 128), 1)
    out = jnp.zeros((ROWS, 128), f32)
    for c, column in enumerate(columns):
        out = jnp.where(lane == line + 32 * c, column, out)
    return jnp.sum(out, axis=0, keepdims=True)


def spread_kernel(ids, recv, disp, energy, mass, out):
    owner, _, gy = place(ids)
    chunk = recv[owner // NGY].astype(f32)
    coords = rows_of([chunk[r, c : c + 1] for c in range(2) for r in range(4)])

    def edge(at):
        cut = slice(at, at + 1)
        return column_row([disp[0, :, cut], disp[1, :, cut], energy[:, cut] * mass[:, cut]])

    head, tail = edge(0), edge(COLS - 1)
    after = lax.rem(gy + 1, NGY)
    for z in range(NGY):
        line = jnp.where(after == z, tail, head)
        low = rows_of([line, chunk[z // 4, 2:3], chunk[z // 4, 3:4]])
        out[z] = jnp.concatenate([coords, low], axis=0).astype(bf16)


def gather_kernel(ids, recv, disp, energy, mass, out, sides, impulse):
    owner, gx, gy = place(ids)
    picked = recv[lax.rem(owner, NGY)].astype(f32)
    left = recv[lax.rem(gy + NGY - 1, NGY)].astype(f32)[8:9]
    right = recv[lax.rem(gy + 1, NGY)].astype(f32)[8:9]
    coords = picked[0:8]
    sides[...] = rows_of([left, right])
    impulse[...] = rows_of([picked[9:10], picked[10:11]])

    def edge(at):
        cut = slice(at, at + 1)
        fields = (disp[0, cut], disp[1, cut], energy[cut] * mass[cut])
        return rows_of([f[:, h : h + 128] for f in fields for h in (0, 128)] + [left, right])

    tail = jnp.concatenate([coords, edge(ROWS - 1)], axis=0).astype(bf16)
    head = jnp.concatenate([coords, edge(0)], axis=0).astype(bf16)
    for d in range(NGX):
        out[d] = head
    out[lax.rem(gx + 1, NGX)] = tail


def zone_forces(ids, recv, sides, disp, energy, mass, field, force):
    _, gx, gy = place(ids)
    above = recv[lax.rem(gx + NGX - 1, NGX)].astype(f32)[8:16]
    below = recv[lax.rem(gx + 1, NGX)].astype(f32)[8:16]
    row8, lane8 = iota((8, 128), 0), iota((8, 128), 1)
    line, lane = iota((ROWS, 128), 0), iota((ROWS, 128), 1)
    lane1 = iota((1, 128), 1)

    def corner(rows, k, at):
        return jnp.sum(jnp.where(lane1 == at, rows[k : k + 1], 0.0), axis=1, keepdims=True)

    for c in range(3):
        own = energy[...] * mass[...] if c == 2 else disp[c]
        field[c, 0:ROWS, 0:COLS] = own
        for h in range(2):
            k = 2 * c + h
            field[c, ROWS : ROWS + 8, 128 * h : 128 * h + 128] = jnp.where(
                row8 == 0, below[k : k + 1], jnp.where(row8 == 7, above[k : k + 1], 0.0)
            )
        cols = [
            jnp.sum(jnp.where(lane == line + 32 * c, sides[k : k + 1], 0.0), axis=1, keepdims=True)
            for k in range(2)
        ]
        field[c, 0:ROWS, COLS : COLS + 128] = jnp.where(
            lane == 0, cols[1], jnp.where(lane == 127, cols[0], 0.0)
        )
        first, last = 32 * c, 32 * c + 31
        low = jnp.where(
            lane8 == 0, corner(below, 7, first), jnp.where(lane8 == 127, corner(below, 6, first), 0.0)
        )
        high = jnp.where(
            lane8 == 0, corner(above, 7, last), jnp.where(lane8 == 127, corner(above, 6, last), 0.0)
        )
        field[c, ROWS : ROWS + 8, COLS : COLS + 128] = jnp.where(
            row8 == 0, low, jnp.where(row8 == 7, high, 0.0)
        )

    height, width = ROWS + 8, COLS + 128

    def next_row(v):
        return pltpu.roll(v, height - 1, 0)

    def next_col(v):
        return pltpu.roll(v, width - 1, 1)

    def prev_row(v):
        return pltpu.roll(v, 1, 0)

    def prev_col(v):
        return pltpu.roll(v, 1, 1)

    first, second = [], []
    for c in range(2):
        a = field[c]
        b = next_row(a)
        first.append(next_col(b) - a + 1.0)
        second.append(next_col(a) - b + (-1.0 if c == 0 else 1.0))
    at_row, at_col = iota((height, width), 0), iota((height, width), 1)
    zone_row = jnp.where(at_row == height - 1, -1, at_row)
    zone_col = jnp.where(at_col == width - 1, -1, at_col)
    in_row, in_col = gx * ROWS + zone_row, gy * COLS + zone_col
    live = (
        (zone_row < ROWS)
        & (zone_col < COLS)
        & (in_row >= 0)
        & (in_row < TOTAL_ROWS - 1)
        & (in_col >= 0)
        & (in_col < TOTAL_COLS - 1)
    )
    area = jnp.where(live, 0.5 * (first[0] * second[1] - second[0] * first[1]), 1.0)
    press = jnp.where(live, 0.2 * field[2] / area, 0.0)
    on_a = (-press * second[1], press * second[0])
    on_b = (press * first[1], -press * first[0])
    for c in range(2):
        total = (on_a[c] - prev_col(on_b[c])) + prev_row(on_b[c] - prev_col(on_a[c]))
        force[c] = total[0:ROWS, 0:COLS]
    scale = jnp.where(
        live[0:ROWS, 0:COLS], jnp.sqrt(area[0:ROWS, 0:COLS]) / jnp.sqrt(0.56 * energy[...]), 1e30
    )
    least = jnp.min(scale, axis=0, keepdims=True)
    return jnp.minimum(least[:, 0:128], least[:, 128:256])


def contact_terms(slave_x, slave_y, start_x, start_y, end_x, end_y, side, live):
    rel_x = slave_x - start_x + 0.5
    rel_y = slave_y - start_y
    along_x = 1.0 + end_x - start_x
    along_y = end_y - start_y
    along_sq = along_x * along_x + along_y * along_y
    length = jnp.sqrt(along_sq)
    fraction = (rel_x * along_x + rel_y * along_y) / along_sq
    normal_x = -along_y / length
    normal_y = along_x / length
    gap_size = normal_x * rel_x + normal_y * rel_y
    sign = 1.0 - 2.0 * side.astype(f32)
    depth = -sign * gap_size / GAP_SCALE
    soft = jnp.maximum(depth, 0.0) + jnp.log1p(jnp.exp(-jnp.abs(depth)))
    magnitude = jnp.where(live, STIFFNESS * GAP_SCALE * soft, 0.0)
    return magnitude * sign * normal_x, magnitude * sign * normal_y, magnitude, fraction


def high_low(v):
    high = v.astype(bf16).astype(f32)
    return high, v - high


def contact_kernel(
    ids,
    count,
    recv,
    sides,
    disp,
    energy,
    mass,
    pair_node,
    pair_segment,
    pair_side,
    out,
    force,
    field,
    nodes,
    picks,
    reaction,
    pushed,
):
    least = zone_forces(ids, recv, sides, disp, energy, mass, field, force)
    coords = recv[...].astype(f32)[:, 0:8].reshape(8 * NGX, 128).astype(bf16)
    for c in range(2):
        for h in range(2):
            rest = disp[c, :, 128 * h : 128 * h + 128]
            for k in range(3):
                high, low = high_low(rest)
                at = 128 * k + 64 * c + 32 * h
                nodes[at : at + 32] = high.astype(bf16)
                rest = low
    reaction[...] = jnp.zeros_like(reaction)
    pushed[...] = jnp.zeros_like(pushed)
    live_count = count[0]

    def block(index, carry):
        begin = pl.multiple_of(index * BLOCK, BLOCK)
        cut = (slice(None), pl.ds(begin, BLOCK))
        segment = pair_segment[cut]
        ends = jnp.concatenate([segment, segment + 1], axis=1)
        end_lane = (iota((128, 2 * BLOCK), 0) == (ends & 127)).astype(f32).astype(bf16)
        end_group, end_row = ends >> 9, (ends >> 7) & 3
        looked = jnp.dot(coords, end_lane, preferred_element_type=f32)
        found = jnp.zeros((8, 2 * BLOCK), f32)
        for s in range(NGX):
            found = found + jnp.where(end_group == s, looked[8 * s : 8 * s + 8], 0.0)
        row8 = iota((8, 2 * BLOCK), 0)
        end_x = jnp.sum(jnp.where(row8 == end_row, found, 0.0), axis=0, keepdims=True)
        end_y = jnp.sum(jnp.where(row8 == end_row + 4, found, 0.0), axis=0, keepdims=True)

        node = pair_node[cut]
        node_lane = (iota((128, BLOCK), 0) == (node & 127)).astype(f32).astype(bf16)
        node_mask = iota((64, BLOCK), 0) == (((node >> 7) & 1) * 32 + (node >> 8))
        seen = jnp.dot(nodes[...], node_lane, preferred_element_type=f32)
        seen = (seen[256:384] + seen[128:256]) + seen[0:128]
        slave_x = jnp.sum(jnp.where(node_mask, seen[0:64], 0.0), axis=0, keepdims=True)
        slave_y = jnp.sum(jnp.where(node_mask, seen[64:128], 0.0), axis=0, keepdims=True)

        live = begin + iota((1, BLOCK), 1) < live_count
        push_x, push_y, magnitude, fraction = contact_terms(
            slave_x,
            slave_y,
            end_x[:, :BLOCK],
            end_y[:, :BLOCK],
            end_x[:, BLOCK:],
            end_y[:, BLOCK:],
            pair_side[cut],
            live,
        )
        share = jnp.concatenate([1.0 - fraction, fraction], axis=1)
        terms = [
            share * jnp.concatenate([v, v], axis=1) for v in (-push_x, -push_y, magnitude)
        ]
        row16 = iota((16, 2 * BLOCK), 0)
        stacked = jnp.where(row16 < 4, terms[0], jnp.where(row16 < 8, terms[1], terms[2]))
        stacked = jnp.where((row16 < 12) & ((row16 & 3) == end_row), stacked, 0.0)
        high, low = high_low(stacked)
        for s in range(NGX):
            mine = end_group == s
            picks[16 * s : 16 * s + 16] = jnp.where(mine, high, 0.0).astype(bf16)
            picks[512 + 16 * s : 528 + 16 * s] = jnp.where(mine, low, 0.0).astype(bf16)
        contract = (((1,), (1,)), ((), ()))
        part = lax.dot_general(picks[...], end_lane, contract, preferred_element_type=f32)
        reaction[...] += part[0:512] + part[512:1024]

        rows = [jnp.where(node_mask, half, 0.0) for v in (push_x, push_y) for half in high_low(v)]
        rows = jnp.concatenate([rows[0], rows[2], rows[1], rows[3]], axis=0).astype(bf16)
        part = lax.dot_general(rows, node_lane, contract, preferred_element_type=f32)
        pushed[...] += part[0:128] + part[128:256]
        return carry

    lax.fori_loop(0, (live_count + BLOCK - 1) // BLOCK, block, 0)
    for c in range(2):
        for h in range(2):
            at = 64 * c + 32 * h
            force[c, :, 128 * h : 128 * h + 128] += pushed[at : at + 32]
    row16 = iota((16, 128), 0)
    for s in range(NGX):
        out[s] = jnp.where(row16 == 12, least, reaction[16 * s : 16 * s + 16])


def sum_kernel(recv, out):
    total = recv[0]
    least = recv[0]
    for s in range(1, NGX):
        part = recv[s]
        total = total + part
        least = jnp.minimum(least, part)
    for q in range(4):
        rows = [total[4 * c + q : 4 * c + q + 1] for c in range(3)] + [least[12:13]]
        tile = rows_of(rows)
        for z in range(4 * q, 4 * q + 4):
            out[z] = tile


def step_kernel(recv, impulse, force, vel, disp, mass, new_vel, new_disp, master):
    gy = lax.axis_index("gy")
    finish(gy, recv, impulse, force, vel, disp, mass, new_vel, new_disp, master)


def finish(gy, recv, impulse, force, vel, disp, mass, new_vel, new_disp, master):
    total = recv[0]
    least = recv[0]
    for z in range(1, NGY):
        part = recv[z]
        total = total + part
        least = jnp.minimum(least, part)
    step = 0.3 * jnp.min(least[3:4], axis=1, keepdims=True)
    for c in range(2):
        vel_c = vel[c] + step * force[c] / mass[...]
        new_vel[c] = vel_c
        new_disp[c] = disp[c] + step * vel_c
    shifted = pltpu.roll(impulse[...] + step * total, lax.rem(128 - 32 * lax.rem(gy, 4), 128), 1)
    master[...] = shifted[0:3, 0:32]


def call(kernel, out, ins, scratch=()):
    return pl.pallas_call(
        kernel,
        out_shape=[jax.ShapeDtypeStruct(s, d) for s, d in out],
        in_specs=[SMEM if i == "s" else VMEM for i in ins],
        out_specs=[VMEM] * len(out),
        scratch_shapes=[pltpu.VMEM(s, d) for s, d in scratch],
    )


def exchange(value, axes):
    return lax.all_to_all(value, axes, 0, 0, tiled=True)


def tiles_of(master_block):
    return master_block[0].reshape(4, NGX, 4, 128).transpose(1, 2, 0, 3)


def stages(
    exchange,
    node_disp,
    node_vel,
    node_mass,
    zone_mass,
    zone_energy,
    master_block,
    owner,
    pair_node,
    pair_segment,
    pair_side,
    pair_count,
):
    fields = (node_disp, zone_energy, zone_mass)
    tiles = exchange(tiles_of(master_block), GX)
    (sent,) = call(spread_kernel, [((NGY, 16, 128), bf16)], "svvvv")(owner, tiles, *fields)
    sent = exchange(sent, "gy")
    sent, sides, impulse = call(
        gather_kernel,
        [((NGX, 16, 128), bf16), ((8, 128), f32), ((8, 128), f32)],
        "svvvv",
    )(owner, sent, *fields)
    sent = exchange(sent, GX)
    sent, force = call(
        contact_kernel,
        [((NGX, 16, 128), f32), ((2, ROWS, COLS), f32)],
        "ssvvvvvvvv",
        [
            ((3, ROWS + 8, COLS + 128), f32),
            ((384, 128), bf16),
            ((1024, 2 * BLOCK), bf16),
            ((512, 128), f32),
            ((128, 128), f32),
        ],
    )(owner, pair_count, sent, sides, *fields, pair_node, pair_segment, pair_side)
    sent = exchange(sent, GX)
    (sent,) = call(sum_kernel, [((NGY, 8, 128), f32)], "v")(sent)
    sent = exchange(sent, "gy")
    return tuple(
        call(
            step_kernel,
            [((2, ROWS, COLS), f32), ((2, ROWS, COLS), f32), ((3, 32), f32)],
            "vvvvvv",
        )(sent, impulse, force, node_vel, node_disp, node_mass)
    )


def shards(*args):
    return stages(exchange, *args)


def solution(mesh):
    split = Mesh(mesh.devices.reshape(4, 4, 2, mesh.shape["gy"]), ("gx_0", "gx_1", "gx_2", "gy"))
    in_specs = (
        P(None, GX, "gy"),
        P(None, GX, "gy"),
        P(GX, "gy"),
        P(GX, "gy"),
        P(GX, "gy"),
        P(GX_GY, None, None),
        P(),
        P(GX_GY, None),
        P(GX_GY, None),
        P(GX_GY, None),
        P(GX_GY),
    )
    out_specs = (P(None, GX, "gy"), P(None, GX, "gy"), P(None, GX_GY))
    return jax.shard_map(
        shards, mesh=split, in_specs=in_specs, out_specs=out_specs, check_vma=False
    )
```

time: 806 us -> 98.7 us (0.12)
  the two profiles are of different devices: /device:TPU:4 before, /device:TPU:1 now
where the time goes in v1:
time: 98.7 us; the launch traced here: 98.5 us
  blocking collectives  55.4 us (56%)
  starting transfers between devices  16 us (16%)
  waiting for transfers between devices  14.3 us (14%)
  Pallas kernels  9.5 us (10%)
  between operations  1.95 us (2%)
  local copies, waits for them, and re-layouts  1.3 us (1%)
    all_to_all x3, blocking collectives, exchange(): return lax.all_to_all(value, axes, 0, 0, tiled=True)  55.4 us
    all_to_all x2, starting transfers between devices, exchange(): return lax.all_to_all(value, axes, 0, 0, tiled=True)  16 us
    all_to_all x2, waiting for transfers between devices, exchange(): return lax.all_to_all(value, axes, 0, 0, tiled=True)  14.3 us
    pallas_call x1, Pallas kernels, stages(): call(contact_kernel, [((NGX, 16, 128), f32), ((2, ROWS, COLS), f32)], 'ss...  2.93 us
  transfers between devices with their start and end apart: 2, of which 2 were waited for; matrix products, arithmetic and copies ran while one was open for 0% of the time, Pallas kernels for 0%

profile of v1, /device:TPU:1, one launch (start us, length us, event | category | flops | bytes accessed | tf_op | source)
XLA Modules:
  0.0 98.5 jit_solution(5857194783203420995)
XLA Ops:
  0.6 10.4 %all-to-all-start = ((bf16[32,4,4,128]{3,2,1,0:T(4,128)(2,1)}), bf16[32,4,4,128]{3,2,1,0:T(4,128)(2,1)S(1)}, u32[]{:S(2)}, u32[]{:S(2)}) async-start(bf16[32,4,4,128]{3,2,1,0:T(4,128)(2,1)} %bitcast.3), calls=%async_computation | async-start | bytes 262144 | tf_op jit(solution)/shard_map/all_to_all | solution.py:341
  11.6 7.1 %all-to-all-done.recv = bf16[32,4,4,128]{3,2,1,0:T(4,128)(2,1)S(1)} async-done(((bf16[32,4,4,128]{3,2,1,0:T(4,128)(2,1)}), bf16[32,4,4,128]{3,2,1,0:T(4,128)(2,1)S(1)}, u32[]{:S(2)}, u32[]{:S(2)}) %all-to-all-start) | async-done | bytes 131104 | tf_op jit(solution)/shard_map/all_to_all | solution.py:341
  18.8 0.0 copy-start
  18.8 0.7 copy-done
  19.4 1.7 %shard_map.130 = bf16[16,16,128]{2,1,0:T(8,128)(2,1)} custom-call(s32[1]{0:T(128)S(6)} %copy.14.ids, bf16[32,4,4,128]{3,2,1,0:T(4,128)(2,1)} %copy-done, f32[2,32,256]{2,1,0:T(8,128)} %disp.7, f32[32,256]{1,0:T(8,128)} %energy.5, f32[32,256]{1,0:T(8,128)} %mass.6), custom_call_target="tpu_custom_call" | custom-call | tf_op jit(solution)/shard_map/pallas_call | solution.py:364
  21.1 24.7 %all_to_all.25.recv = bf16[16,16,128]{2,1,0:T(8,128)(2,1)} all-to-all(bf16[16,16,128]{2,1,0:T(8,128)(2,1)} %shard_map.130), channel_id=1, replica_groups=mesh['gx_0'=4,'gx_1'=4,'gx_2'=2,'gy'=16] {'gy'}, dimensions={0} | all-to-all | bytes 131072 | tf_op jit(solution)/shard_map/all_to_all | solution.py:341
  45.9 1.6 %shard_map.131 = (bf16[32,16,128]{2,1,0:T(8,128)(2,1)}, f32[8,128]{1,0:T(8,128)}, f32[8,128]{1,0:T(8,128)}) custom-call(s32[1]{0:T(128)S(6)} %copy.14.ids, bf16[16,16,128]{2,1,0:T(8,128)(2,1)} %all_to_all.25.recv, f32[2,32,256]{2,1,0:T(8,128)} %disp.7, f32[32,256]{1,0:T(8,128)} %energy.5, f32[32,256]{1,0:T(8,128)} %mass.6), custom_call_target="tpu_custom_call" | custom-call | tf_op jit(solution)/shard_map/pallas_call | solution.py:366
  47.4 5.7 %all-to-all-start.2 = ((bf16[32,16,128]{2,1,0:T(8,128)(2,1)}), bf16[32,16,128]{2,1,0:T(8,128)(2,1)S(1)}, u32[]{:S(2)}, u32[]{:S(2)}) async-start(bf16[32,16,128]{2,1,0:T(8,128)(2,1)} %get-tuple-element.8), calls=%async_computation.2 | async-start | bytes 262144 | tf_op jit(solution)/shard_map/all_to_all | solution.py:341
  53.7 7.1 %all-to-all-done.2.recv = bf16[32,16,128]{2,1,0:T(8,128)(2,1)S(1)} async-done(((bf16[32,16,128]{2,1,0:T(8,128)(2,1)}), bf16[32,16,128]{2,1,0:T(8,128)(2,1)S(1)}, u32[]{:S(2)}, u32[]{:S(2)}) %all-to-all-start.2) | async-done | bytes 131104 | tf_op jit(solution)/shard_map/all_to_all | solution.py:341
  60.9 0.0 copy-start.1
  60.9 0.6 copy-done.1
  61.5 2.9 %shard_map.132 = (f32[32,16,128]{2,1,0:T(8,128)}, f32[2,32,256]{2,1,0:T(8,128)}) custom-call(s32[1]{0:T(128)S(6)} %copy.14.ids, s32[1]{0:T(128)S(6)} %copy.15.count, bf16[32,16,128]{2,1,0:T(8,128)(2,1)} %copy-done.1, f32[8,128]{1,0:T(8,128)} %get-tuple-element.9.sides, f32[2,32,256]{2,1,0:T(8,128)} %disp.7, f32[32,256]{1,0:T(8,128)} %energy.5, ...), custom_call_target="tpu_custom_call" | custom-call | tf_op jit(solution)/shard_map/pallas_call | solution.py:372
  64.5 14.9 %all_to_all.26.recv = f32[32,16,128]{2,1,0:T(8,128)} all-to-all(f32[32,16,128]{2,1,0:T(8,128)} %get-tuple-element.10), channel_id=1, replica_groups=mesh['gx_0'=4,'gx_1'=4,'gx_2'=2,'gy'=16] {'gx_0','gx_1','gx_2'}, dimensions={0} | all-to-all | bytes 524288 | tf_op jit(solution)/shard_map/all_to_all | solution.py:341
  79.4 1.6 %shard_map.133 = f32[16,8,128]{2,1,0:T(8,128)} custom-call(f32[32,16,128]{2,1,0:T(8,128)} %all_to_all.26.recv), custom_call_target="tpu_custom_call" | custom-call | tf_op jit(solution)/shard_map/pallas_call | solution.py:385
  81.0 15.8 %all_to_all.27.recv = f32[16,8,128]{2,1,0:T(8,128)} all-to-all(f32[16,8,128]{2,1,0:T(8,128)} %shard_map.133), channel_id=1, replica_groups=mesh['gx_0'=4,'gx_1'=4,'gx_2'=2,'gy'=16] {'gy'}, dimensions={0} | all-to-all | bytes 131072 | tf_op jit(solution)/shard_map/all_to_all | solution.py:341
  96.8 1.7 %shard_map.134 = (f32[2,32,256]{2,1,0:T(8,128)}, f32[2,32,256]{2,1,0:T(8,128)}, f32[3,32]{1,0:T(4,128)}) custom-call(f32[16,8,128]{2,1,0:T(8,128)} %all_to_all.27.recv, f32[8,128]{1,0:T(8,128)} %get-tuple-element.11.impulse, f32[2,32,256]{2,1,0:T(8,128)} %get-tuple-element.12.force, f32[2,32,256]{2,1,0:T(8,128)} %vel.1, f32[2,32,256]{2,1,0:T(8,128)} %disp.7, ...), custom_call_target="tpu_custom_call" | custom-call | tf_op jit(solution)/shard_map/pallas_call | solution.py:388
Async XLA Ops:
  0.6 18.2 %all-to-all-start = ((bf16[32,4,4,128]{3,2,1,0:T(4,128)(2,1)}), bf16[32,4,4,128]{3,2,1,0:T(4,128)(2,1)S(1)}, u32[]{:S(2)}, u32[]{:S(2)}) async-start(bf16[32,4,4,128]{3,2,1,0:T(4,128)(2,1)} %bitcast.3), calls=%async_computation | async-start | bytes 262144 | tf_op jit(solution)/shard_map/all_to_all | solution.py:341
  18.8 0.7 copy-start
  47.4 13.5 %all-to-all-start.2 = ((bf16[32,16,128]{2,1,0:T(8,128)(2,1)}), bf16[32,16,128]{2,1,0:T(8,128)(2,1)S(1)}, u32[]{:S(2)}, u32[]{:S(2)}) async-start(bf16[32,16,128]{2,1,0:T(8,128)(2,1)} %get-tuple-element.8), calls=%async_computation.2 | async-start | bytes 262144 | tf_op jit(solution)/shard_map/all_to_all | solution.py:341
  60.9 0.7 copy-start.1

commit v2 on v1

--- a/solution.py
+++ b/solution.py
@@ -334,6 +334,7 @@
         in_specs=[SMEM if i == "s" else VMEM for i in ins],
         out_specs=[VMEM] * len(out),
         scratch_shapes=[pltpu.VMEM(s, d) for s, d in scratch],
+        compiler_params=pltpu.CompilerParams(vmem_limit_bytes=16 << 20),
     )
 
 

time: 98.7 us -> 89.4 us (0.906)
  Pallas kernels: 9.5 us -> 2.82 us
  blocking collectives: 55.4 us -> 53.5 us
  local copies, waits for them, and re-layouts: 1.3 us -> 0.04 us
    all_to_all x3, blocking collectives: 55.4 us -> 53.5 us  [exchange(): return lax.all_to_all(value, axes, 0, 0, tiled=True)]
    pallas_call x1, Pallas kernels: 2.93 us -> 1.23 us  [stages(): call(contact_kernel, [((NGX, 16, 128), f32), ((2, ROWS, COLS), f32)], 'ss...]
    pallas_call x1, Pallas kernels: 1.62 us -> 0.04 us  [stages(): sent, = call(sum_kernel, [((NGY, 8, 128), f32)], 'v')(sent)]
    pallas_call x1, Pallas kernels: 1.7 us -> 0.12 us  [stages(): call(spread_kernel, [((NGY, 16, 128), bf16)], 'svvvv')]
    unnamed x4 -> x16, local copies, waits for them, and re-layouts: 1.3 us -> 0.04 us
where the time goes in v2:
time: 89.4 us; the launch traced here: 89 us
  blocking collectives  53.5 us (60%)
  starting transfers between devices  16.3 us (18%)
  waiting for transfers between devices  14.3 us (16%)
  Pallas kernels  2.82 us (3%)
  between operations  2.01 us (2%)
    all_to_all x3, blocking collectives, exchange(): return lax.all_to_all(value, axes, 0, 0, tiled=True)  53.5 us
    all_to_all x2, starting transfers between devices, exchange(): return lax.all_to_all(value, axes, 0, 0, tiled=True)  16.3 us
    all_to_all x2, waiting for transfers between devices, exchange(): return lax.all_to_all(value, axes, 0, 0, tiled=True)  14.3 us
  transfers between devices with their start and end apart: 2, of which 2 were waited for; matrix products, arithmetic and copies ran while one was open for 0% of the time, Pallas kernels for 0%

profile of v2, /device:TPU:1, one launch (start us, length us, event | category | flops | bytes accessed | tf_op | source)
XLA Modules:
  0.0 89.0 jit_solution(3242995017420140933)
XLA Ops:
  0.6 0.0 copy-start
  0.6 0.0 copy-start.1
  0.7 0.0 copy-start.2
  0.7 10.5 %all-to-all-start = ((bf16[32,4,4,128]{3,2,1,0:T(4,128)(2,1)}), bf16[32,4,4,128]{3,2,1,0:T(4,128)(2,1)S(1)}, u32[]{:S(2)}, u32[]{:S(2)}) async-start(bf16[32,4,4,128]{3,2,1,0:T(4,128)(2,1)} %bitcast.3), calls=%async_computation | async-start | bytes 262144 | tf_op jit(solution)/shard_map/all_to_all | solution.py:342
  11.8 7.1 %all-to-all-done.recv = bf16[32,4,4,128]{3,2,1,0:T(4,128)(2,1)S(1)} async-done(((bf16[32,4,4,128]{3,2,1,0:T(4,128)(2,1)}), bf16[32,4,4,128]{3,2,1,0:T(4,128)(2,1)S(1)}, u32[]{:S(2)}, u32[]{:S(2)}) %all-to-all-start) | async-done | bytes 131104 | tf_op jit(solution)/shard_map/all_to_all | solution.py:342
  19.0 0.0 copy-done
  19.0 0.0 copy-done.1
  19.0 0.0 copy-done.2
  19.0 0.1 shard_map.130
  19.1 24.4 %all_to_all.25.recv = bf16[16,16,128]{2,1,0:T(8,128)(2,1)S(1)} all-to-all(bf16[16,16,128]{2,1,0:T(8,128)(2,1)S(1)} %shard_map.130), channel_id=1, replica_groups=mesh['gx_0'=4,'gx_1'=4,'gx_2'=2,'gy'=16] {'gy'}, dimensions={0} | all-to-all | bytes 131072 | tf_op jit(solution)/shard_map/all_to_all | solution.py:342
  43.5 0.7 shard_map.131
  44.2 0.0 copy-start.5
  44.2 0.0 copy-start.6
  44.2 0.0 copy-start.7
  44.2 5.8 %all-to-all-start.2 = ((bf16[32,16,128]{2,1,0:T(8,128)(2,1)}), bf16[32,16,128]{2,1,0:T(8,128)(2,1)S(1)}, u32[]{:S(2)}, u32[]{:S(2)}) async-start(bf16[32,16,128]{2,1,0:T(8,128)(2,1)} %get-tuple-element.8), calls=%async_computation.2 | async-start | bytes 262144 | tf_op jit(solution)/shard_map/all_to_all | solution.py:342
  50.7 7.1 %all-to-all-done.2.recv = bf16[32,16,128]{2,1,0:T(8,128)(2,1)S(1)} async-done(((bf16[32,16,128]{2,1,0:T(8,128)(2,1)}), bf16[32,16,128]{2,1,0:T(8,128)(2,1)S(1)}, u32[]{:S(2)}, u32[]{:S(2)}) %all-to-all-start.2) | async-done | bytes 131104 | tf_op jit(solution)/shard_map/all_to_all | solution.py:342
  57.8 0.0 copy-done.5
  57.8 0.0 copy-done.6
  57.8 0.0 copy-done.7
  57.8 1.2 %shard_map.132 = (f32[32,16,128]{2,1,0:T(8,128)S(1)}, f32[2,32,256]{2,1,0:T(8,128)S(1)}) custom-call(s32[1]{0:T(128)S(6)} %copy.14.ids, s32[1]{0:T(128)S(6)} %copy.15.count, bf16[32,16,128]{2,1,0:T(8,128)(2,1)S(1)} %all-to-all-done.2.recv, f32[8,128]{1,0:T(8,128)S(1)} %get-tuple-element.9.sides, f32[2,32,256]{2,1,0:T(8,128)S(1)} %copy-done, ...), custom_call_target="tpu_custom_call" | custom-call | tf_op jit(solution)/shard_map/pallas_call | solution.py:373
  59.0 13.9 %all_to_all.26.recv = f32[32,16,128]{2,1,0:T(8,128)S(1)} all-to-all(f32[32,16,128]{2,1,0:T(8,128)S(1)} %get-tuple-element.10), channel_id=1, replica_groups=mesh['gx_0'=4,'gx_1'=4,'gx_2'=2,'gy'=16] {'gx_0','gx_1','gx_2'}, dimensions={0} | all-to-all | bytes 524288 | tf_op jit(solution)/shard_map/all_to_all | solution.py:342
  73.0 0.0 copy-start.3
  73.0 0.0 copy-start.4
  73.0 15.2 %all_to_all.27.recv = f32[16,8,128]{2,1,0:T(8,128)S(1)} all-to-all(f32[16,8,128]{2,1,0:T(8,128)S(1)} %shard_map.133), channel_id=1, replica_groups=mesh['gx_0'=4,'gx_1'=4,'gx_2'=2,'gy'=16] {'gy'}, dimensions={0} | all-to-all | bytes 131072 | tf_op jit(solution)/shard_map/all_to_all | solution.py:342
  88.2 0.0 copy-done.3
  88.2 0.0 copy-done.4
  88.2 0.8 shard_map.134
  (1 shorter events, 0.0 us)
Async XLA Ops:
  0.6 18.3 %copy-start = (f32[2,32,256]{2,1,0:T(8,128)S(1)}, f32[2,32,256]{2,1,0:T(8,128)}, u32[]{:S(2)}) copy-start(f32[2,32,256]{2,1,0:T(8,128)} %disp.7) | copy-start | bytes 196612
  0.6 18.3 %copy-start.1 = (f32[32,256]{1,0:T(8,128)S(1)}, f32[32,256]{1,0:T(8,128)}, u32[]{:S(2)}) copy-start(f32[32,256]{1,0:T(8,128)} %energy.5) | copy-start | bytes 98308
  0.7 18.3 %copy-start.2 = (f32[32,256]{1,0:T(8,128)S(1)}, f32[32,256]{1,0:T(8,128)}, u32[]{:S(2)}) copy-start(f32[32,256]{1,0:T(8,128)} %mass.6) | copy-start | bytes 98308
  0.7 18.3 %all-to-all-start = ((bf16[32,4,4,128]{3,2,1,0:T(4,128)(2,1)}), bf16[32,4,4,128]{3,2,1,0:T(4,128)(2,1)S(1)}, u32[]{:S(2)}, u32[]{:S(2)}) async-start(bf16[32,4,4,128]{3,2,1,0:T(4,128)(2,1)} %bitcast.3), calls=%async_computation | async-start | bytes 262144 | tf_op jit(solution)/shard_map/all_to_all | solution.py:342
  44.2 13.6 %copy-start.5 = (s32[1,1024]{1,0:T(1,128)S(1)}, s32[1,1024]{1,0:T(1,128)}, u32[]{:S(2)}) copy-start(s32[1,1024]{1,0:T(1,128)} %pair_node.1) | copy-start | bytes 12292
  44.2 13.6 %copy-start.6 = (s32[1,1024]{1,0:T(1,128)S(1)}, s32[1,1024]{1,0:T(1,128)}, u32[]{:S(2)}) copy-start(s32[1,1024]{1,0:T(1,128)} %pair_segment.1) | copy-start | bytes 12292
  44.2 13.6 %copy-start.7 = (s32[1,1024]{1,0:T(1,128)S(1)}, s32[1,1024]{1,0:T(1,128)}, u32[]{:S(2)}) copy-start(s32[1,1024]{1,0:T(1,128)} %pair_side.1) | copy-start | bytes 12292
  44.2 13.6 %all-to-all-start.2 = ((bf16[32,16,128]{2,1,0:T(8,128)(2,1)}), bf16[32,16,128]{2,1,0:T(8,128)(2,1)S(1)}, u32[]{:S(2)}, u32[]{:S(2)}) async-start(bf16[32,16,128]{2,1,0:T(8,128)(2,1)} %get-tuple-element.8), calls=%async_computation.2 | async-start | bytes 262144 | tf_op jit(solution)/shard_map/all_to_all | solution.py:342
  73.0 15.2 %copy-start.3 = (f32[2,32,256]{2,1,0:T(8,128)S(1)}, f32[2,32,256]{2,1,0:T(8,128)}, u32[]{:S(2)}) copy-start(f32[2,32,256]{2,1,0:T(8,128)} %vel.1) | copy-start | bytes 196612
  73.0 15.2 %copy-start.4 = (f32[32,256]{1,0:T(8,128)S(1)}, f32[32,256]{1,0:T(8,128)}, u32[]{:S(2)}) copy-start(f32[32,256]{1,0:T(8,128)} %mass.7) | copy-start | bytes 98308

commit v3 on v2

--- a/solution.py
+++ b/solution.py
@@ -49,31 +49,32 @@
     return jnp.sum(out, axis=0, keepdims=True)
 
 
-def spread_kernel(ids, recv, disp, energy, mass, out):
-    owner, _, gy = place(ids)
-    chunk = recv[owner // NGY].astype(f32)
-    coords = rows_of([chunk[r, c : c + 1] for c in range(2) for r in range(4)])
+def spread_kernel(ids, chunk, disp, energy, mass, out):
+    _, _, gy = place(ids)
+    for h in range(2):
+        rows = [chunk[2 * r + h, c : c + 1].astype(f32) for c in range(2) for r in range(2)]
+        coords = rows_of(rows)[0:4].astype(bf16)
+        for z in range(NGY):
+            out[z, h] = coords
 
     def edge(at):
         cut = slice(at, at + 1)
-        return column_row([disp[0, :, cut], disp[1, :, cut], energy[:, cut] * mass[:, cut]])
+        columns = [disp[0, :, cut], disp[1, :, cut], energy[:, cut] * mass[:, cut]]
+        return rows_of([column_row(columns)])[0:4].astype(bf16)
 
     head, tail = edge(0), edge(COLS - 1)
-    after = lax.rem(gy + 1, NGY)
     for z in range(NGY):
-        line = jnp.where(after == z, tail, head)
-        low = rows_of([line, chunk[z // 4, 2:3], chunk[z // 4, 3:4]])
-        out[z] = jnp.concatenate([coords, low], axis=0).astype(bf16)
-
-
-def gather_kernel(ids, recv, disp, energy, mass, out, sides, impulse):
+        out[z, 2] = head
+    out[lax.rem(gy + 1, NGY), 2] = tail
+
+
+def gather_kernel(ids, recv, disp, energy, mass, out, sides):
     owner, gx, gy = place(ids)
     picked = recv[lax.rem(owner, NGY)].astype(f32)
-    left = recv[lax.rem(gy + NGY - 1, NGY)].astype(f32)[8:9]
-    right = recv[lax.rem(gy + 1, NGY)].astype(f32)[8:9]
-    coords = picked[0:8]
+    left = recv[lax.rem(gy + NGY - 1, NGY), 2].astype(f32)[0:1]
+    right = recv[lax.rem(gy + 1, NGY), 2].astype(f32)[0:1]
+    coords = jnp.concatenate([picked[0], picked[1]], axis=0)
     sides[...] = rows_of([left, right])
-    impulse[...] = rows_of([picked[9:10], picked[10:11]])
 
     def edge(at):
         cut = slice(at, at + 1)
@@ -166,8 +167,7 @@
     scale = jnp.where(
         live[0:ROWS, 0:COLS], jnp.sqrt(area[0:ROWS, 0:COLS]) / jnp.sqrt(0.56 * energy[...]), 1e30
     )
-    least = jnp.min(scale, axis=0, keepdims=True)
-    return jnp.minimum(least[:, 0:128], least[:, 128:256])
+    return jnp.min(scale, axis=0, keepdims=True)
 
 
 def contact_terms(slave_x, slave_y, start_x, start_y, end_x, end_y, side, live):
@@ -193,11 +193,54 @@
     return high, v - high
 
 
+def one_hot(count, index):
+    at = lax.broadcasted_iota(jnp.int32, (count, index.shape[1]), 0).astype(f32).astype(bf16)
+    return jnp.where(at == index.astype(f32).astype(bf16), jnp.ones((), bf16), jnp.zeros((), bf16))
+
+
+def blocks_of(live_count):
+    return (live_count + BLOCK - 1) // BLOCK
+
+
+def block_at(index):
+    begin = pl.multiple_of(index * BLOCK, BLOCK)
+    return begin, (slice(None), pl.ds(begin, BLOCK))
+
+
+def node_place(node):
+    row = ((node >> 7) & 1) * 32 + (node >> 8)
+    return one_hot(128, node & 127), iota((64, BLOCK), 0) == row
+
+
+def slave_kernel(count, disp, pair_node, out, nodes):
+    for c in range(2):
+        for h in range(2):
+            rest = disp[c, :, 128 * h : 128 * h + 128]
+            for k in range(3):
+                high, low = high_low(rest)
+                at = 128 * k + 64 * c + 32 * h
+                nodes[at : at + 32] = high.astype(bf16)
+                rest = low
+
+    def block(index, carry):
+        _, cut = block_at(index)
+        lanes, mask = node_place(pair_node[cut])
+        seen = jnp.dot(nodes[...], lanes, preferred_element_type=f32)
+        seen = (seen[256:384] + seen[128:256]) + seen[0:128]
+        for c in range(2):
+            found = jnp.where(mask, seen[64 * c : 64 * c + 64], 0.0)
+            out[c : c + 1, cut[1]] = jnp.sum(found, axis=0, keepdims=True)
+        return carry
+
+    lax.fori_loop(0, blocks_of(count[0]), block, 0)
+
+
 def contact_kernel(
     ids,
     count,
     recv,
     sides,
+    slaves,
     disp,
     energy,
     mass,
@@ -207,52 +250,42 @@
     out,
     force,
     field,
-    nodes,
+    coords,
     picks,
     reaction,
     pushed,
 ):
     least = zone_forces(ids, recv, sides, disp, energy, mass, field, force)
-    coords = recv[...].astype(f32)[:, 0:8].reshape(8 * NGX, 128).astype(bf16)
-    for c in range(2):
-        for h in range(2):
-            rest = disp[c, :, 128 * h : 128 * h + 128]
-            for k in range(3):
-                high, low = high_low(rest)
-                at = 128 * k + 64 * c + 32 * h
-                nodes[at : at + 32] = high.astype(bf16)
-                rest = low
+    row8 = iota((8, 128), 0)
+    for i in range(NGX // 2):
+        even, odd = recv[2 * i, 0:8].astype(f32), recv[2 * i + 1, 0:8].astype(f32)
+        field[0, 8 * (i % 4) : 8 * (i % 4) + 8, 0:128] = jnp.where(row8 < 4, even, pltpu.roll(odd, 4, 0))
+        field[0, 8 * (i % 4) : 8 * (i % 4) + 8, 128:256] = jnp.where(row8 < 4, pltpu.roll(even, 4, 0), odd)
+        if i % 4 == 3:
+            coords[8 * i - 24 : 8 * i + 8] = field[0, 0:32, 0:256].astype(bf16)
     reaction[...] = jnp.zeros_like(reaction)
     pushed[...] = jnp.zeros_like(pushed)
     live_count = count[0]
 
     def block(index, carry):
-        begin = pl.multiple_of(index * BLOCK, BLOCK)
-        cut = (slice(None), pl.ds(begin, BLOCK))
+        begin, cut = block_at(index)
         segment = pair_segment[cut]
         ends = jnp.concatenate([segment, segment + 1], axis=1)
-        end_lane = (iota((128, 2 * BLOCK), 0) == (ends & 127)).astype(f32).astype(bf16)
-        end_group, end_row = ends >> 9, (ends >> 7) & 3
-        looked = jnp.dot(coords, end_lane, preferred_element_type=f32)
+        lanes = one_hot(256, ends & 255)
+        piece, line = ends >> 9, (ends >> 8) & 1
+        looked = jnp.dot(coords[...], lanes, preferred_element_type=f32)
         found = jnp.zeros((8, 2 * BLOCK), f32)
-        for s in range(NGX):
-            found = found + jnp.where(end_group == s, looked[8 * s : 8 * s + 8], 0.0)
-        row8 = iota((8, 2 * BLOCK), 0)
-        end_x = jnp.sum(jnp.where(row8 == end_row, found, 0.0), axis=0, keepdims=True)
-        end_y = jnp.sum(jnp.where(row8 == end_row + 4, found, 0.0), axis=0, keepdims=True)
-
-        node = pair_node[cut]
-        node_lane = (iota((128, BLOCK), 0) == (node & 127)).astype(f32).astype(bf16)
-        node_mask = iota((64, BLOCK), 0) == (((node >> 7) & 1) * 32 + (node >> 8))
-        seen = jnp.dot(nodes[...], node_lane, preferred_element_type=f32)
-        seen = (seen[256:384] + seen[128:256]) + seen[0:128]
-        slave_x = jnp.sum(jnp.where(node_mask, seen[0:64], 0.0), axis=0, keepdims=True)
-        slave_y = jnp.sum(jnp.where(node_mask, seen[64:128], 0.0), axis=0, keepdims=True)
+        for s in range(NGX // 2):
+            found = found + jnp.where((piece >> 1) == s, looked[8 * s : 8 * s + 8], 0.0)
+        row = iota((8, 2 * BLOCK), 0)
+        at = (piece & 1) * 4 + line
+        end_x = jnp.sum(jnp.where(row == at, found, 0.0), axis=0, keepdims=True)
+        end_y = jnp.sum(jnp.where(row == at + 2, found, 0.0), axis=0, keepdims=True)
 
         live = begin + iota((1, BLOCK), 1) < live_count
         push_x, push_y, magnitude, fraction = contact_terms(
-            slave_x,
-            slave_y,
+            slaves[0:1, cut[1]],
+            slaves[1:2, cut[1]],
             end_x[:, :BLOCK],
             end_y[:, :BLOCK],
             end_x[:, BLOCK:],
@@ -260,74 +293,90 @@
             pair_side[cut],
             live,
         )
+        push_x, push_y = jnp.where(live, push_x, 0.0), jnp.where(live, push_y, 0.0)
+        fraction = jnp.where(live, fraction, 0.0)
         share = jnp.concatenate([1.0 - fraction, fraction], axis=1)
         terms = [
             share * jnp.concatenate([v, v], axis=1) for v in (-push_x, -push_y, magnitude)
         ]
-        row16 = iota((16, 2 * BLOCK), 0)
-        stacked = jnp.where(row16 < 4, terms[0], jnp.where(row16 < 8, terms[1], terms[2]))
-        stacked = jnp.where((row16 < 12) & ((row16 & 3) == end_row), stacked, 0.0)
+        stacked = jnp.where(row < 2, terms[0], jnp.where(row < 4, terms[1], terms[2]))
+        stacked = jnp.where((row < 6) & ((row & 1) == line), stacked, 0.0)
         high, low = high_low(stacked)
-        for s in range(NGX):
-            mine = end_group == s
-            picks[16 * s : 16 * s + 16] = jnp.where(mine, high, 0.0).astype(bf16)
-            picks[512 + 16 * s : 528 + 16 * s] = jnp.where(mine, low, 0.0).astype(bf16)
+        high = jnp.concatenate([high, high], axis=0).astype(bf16)
+        low = jnp.concatenate([low, low], axis=0).astype(bf16)
+        half = iota((16, 2 * BLOCK), 0) >> 3
+        offset = (piece - half).astype(f32).astype(bf16)
+        nothing = jnp.zeros((), bf16)
+        for s in range(NGX // 2):
+            mine = offset == jnp.asarray(2 * s, bf16)
+            picks[16 * s : 16 * s + 16] = jnp.where(mine, high, nothing)
+            picks[256 + 16 * s : 272 + 16 * s] = jnp.where(mine, low, nothing)
         contract = (((1,), (1,)), ((), ()))
-        part = lax.dot_general(picks[...], end_lane, contract, preferred_element_type=f32)
-        reaction[...] += part[0:512] + part[512:1024]
-
-        rows = [jnp.where(node_mask, half, 0.0) for v in (push_x, push_y) for half in high_low(v)]
+        part = lax.dot_general(picks[...], lanes, contract, preferred_element_type=f32)
+        reaction[...] += part[0:256] + part[256:512]
+
+        lanes, mask = node_place(pair_node[cut])
+        rows = [jnp.where(mask, half, 0.0) for v in (push_x, push_y) for half in high_low(v)]
         rows = jnp.concatenate([rows[0], rows[2], rows[1], rows[3]], axis=0).astype(bf16)
-        part = lax.dot_general(rows, node_lane, contract, preferred_element_type=f32)
+        part = lax.dot_general(rows, lanes, contract, preferred_element_type=f32)
         pushed[...] += part[0:128] + part[128:256]
         return carry
 
-    lax.fori_loop(0, (live_count + BLOCK - 1) // BLOCK, block, 0)
+    lax.fori_loop(0, blocks_of(live_count), block, 0)
     for c in range(2):
         for h in range(2):
             at = 64 * c + 32 * h
             force[c, :, 128 * h : 128 * h + 128] += pushed[at : at + 32]
-    row16 = iota((16, 128), 0)
+    row = iota((8, 256), 0)
     for s in range(NGX):
-        out[s] = jnp.where(row16 == 12, least, reaction[16 * s : 16 * s + 16])
-
-
-def sum_kernel(recv, out):
+        out[s] = jnp.where(row == 6, least, reaction[8 * s : 8 * s + 8])
+
+
+def sum_kernel(recv, chunk, out):
     total = recv[0]
     least = recv[0]
     for s in range(1, NGX):
         part = recv[s]
         total = total + part
         least = jnp.minimum(least, part)
-    for q in range(4):
-        rows = [total[4 * c + q : 4 * c + q + 1] for c in range(3)] + [least[12:13]]
-        tile = rows_of(rows)
-        for z in range(4 * q, 4 * q + 4):
-            out[z] = tile
-
-
-def step_kernel(recv, impulse, force, vel, disp, mass, new_vel, new_disp, master):
-    gy = lax.axis_index("gy")
-    finish(gy, recv, impulse, force, vel, disp, mass, new_vel, new_disp, master)
-
-
-def finish(gy, recv, impulse, force, vel, disp, mass, new_vel, new_disp, master):
+    least = jnp.min(least[6:7], axis=1, keepdims=True)
+    lane = iota((1, 128), 1)
+    for z in range(NGY):
+        rows = total[:, 128 * ((z % 8) // 4) : 128 * ((z % 8) // 4) + 128]
+        line = jnp.broadcast_to(least, (1, 128))
+        old = jnp.zeros((1, 128), f32)
+        for c in range(3):
+            shift = 32 * ((c - z) % 4)
+            mine = (lane >= 32 * c) & (lane < 32 * c + 32)
+            row = rows[2 * c + z // 8 : 2 * c + z // 8 + 1]
+            line = jnp.where(mine, pltpu.roll(row, shift, 1) if shift else row, line)
+            if c < 2:
+                row = chunk[z // 4, 2 + c : 3 + c].astype(f32)
+                old = jnp.where(mine, pltpu.roll(row, shift, 1) if shift else row, old)
+        out[z, 0:1] = line
+        out[z, 1:2] = old
+
+
+def step_kernel(recv, force, vel, disp, mass, new_vel, new_disp, master):
     total = recv[0]
     least = recv[0]
     for z in range(1, NGY):
         part = recv[z]
         total = total + part
         least = jnp.minimum(least, part)
-    step = 0.3 * jnp.min(least[3:4], axis=1, keepdims=True)
+    lane = iota((1, 128), 1)
+    least = jnp.where(lane >= 96, least[0:1], 1e30)
+    step = 0.3 * jnp.min(least, axis=1, keepdims=True)
     for c in range(2):
         vel_c = vel[c] + step * force[c] / mass[...]
         new_vel[c] = vel_c
         new_disp[c] = disp[c] + step * vel_c
-    shifted = pltpu.roll(impulse[...] + step * total, lax.rem(128 - 32 * lax.rem(gy, 4), 128), 1)
-    master[...] = shifted[0:3, 0:32]
-
-
-def call(kernel, out, ins, scratch=()):
+    moved = total[1:2] + step * total[0:1]
+    for c in range(3):
+        master[c : c + 1, :] = moved[:, 32 * c : 32 * c + 32]
+
+
+def call(kernel, out, ins, scratch=(), flops=1_000_000):
     return pl.pallas_call(
         kernel,
         out_shape=[jax.ShapeDtypeStruct(s, d) for s, d in out],
@@ -335,6 +384,7 @@
         out_specs=[VMEM] * len(out),
         scratch_shapes=[pltpu.VMEM(s, d) for s, d in scratch],
         compiler_params=pltpu.CompilerParams(vmem_limit_bytes=16 << 20),
+        cost_estimate=pl.CostEstimate(flops=flops, bytes_accessed=1 << 20, transcendentals=0),
     )
 
 
@@ -342,8 +392,13 @@
     return lax.all_to_all(value, axes, 0, 0, tiled=True)
 
 
-def tiles_of(master_block):
-    return master_block[0].reshape(4, NGX, 4, 128).transpose(1, 2, 0, 3)
+def owner_piece(exchange, master_block, owner):
+    def send():
+        tiles = master_block[0].reshape(4, NGX, 4, 128).transpose(1, 2, 0, 3)
+        return lax.dynamic_index_in_dim(exchange(tiles, GX), owner[0] // NGY, 0, False)
+
+    mine = lax.axis_index("gy") == lax.rem(owner[0], NGY)
+    return lax.cond(mine, send, lambda: jnp.zeros((4, 4, 128), bf16))
 
 
 def stages(
@@ -361,36 +416,37 @@
     pair_count,
 ):
     fields = (node_disp, zone_energy, zone_mass)
-    tiles = exchange(tiles_of(master_block), GX)
-    (sent,) = call(spread_kernel, [((NGY, 16, 128), bf16)], "svvvv")(owner, tiles, *fields)
+    chunk = owner_piece(exchange, master_block, owner)
+    (sent,) = call(spread_kernel, [((NGY, 3, 4, 128), bf16)], "svvvv")(owner, chunk, *fields)
     sent = exchange(sent, "gy")
-    sent, sides, impulse = call(
-        gather_kernel,
-        [((NGX, 16, 128), bf16), ((8, 128), f32), ((8, 128), f32)],
-        "svvvv",
-    )(owner, sent, *fields)
+    sent, sides = call(gather_kernel, [((NGX, 16, 128), bf16), ((8, 128), f32)], "svvvv")(
+        owner, sent, *fields
+    )
+    (slaves,) = call(
+        slave_kernel, [((2, PAIRS), f32)], "svv", [((384, 128), bf16)], flops=100_000_000
+    )(pair_count, node_disp, pair_node)
     sent = exchange(sent, GX)
     sent, force = call(
         contact_kernel,
-        [((NGX, 16, 128), f32), ((2, ROWS, COLS), f32)],
-        "ssvvvvvvvv",
+        [((NGX, 8, 256), f32), ((2, ROWS, COLS), f32)],
+        "ssvvvvvvvvv",
         [
             ((3, ROWS + 8, COLS + 128), f32),
-            ((384, 128), bf16),
-            ((1024, 2 * BLOCK), bf16),
-            ((512, 128), f32),
+            ((128, 256), bf16),
+            ((512, 2 * BLOCK), bf16),
+            ((256, 256), f32),
             ((128, 128), f32),
         ],
-    )(owner, pair_count, sent, sides, *fields, pair_node, pair_segment, pair_side)
+    )(owner, pair_count, sent, sides, slaves, *fields, pair_node, pair_segment, pair_side)
     sent = exchange(sent, GX)
-    (sent,) = call(sum_kernel, [((NGY, 8, 128), f32)], "v")(sent)
+    (sent,) = call(sum_kernel, [((NGY, 2, 128), f32)], "vv")(sent, chunk)
     sent = exchange(sent, "gy")
     return tuple(
         call(
             step_kernel,
             [((2, ROWS, COLS), f32), ((2, ROWS, COLS), f32), ((3, 32), f32)],
-            "vvvvvv",
-        )(sent, impulse, force, node_vel, node_disp, node_mass)
+            "vvvvv",
+        )(sent, force, node_vel, node_disp, node_mass)
     )
 
 

time: 89.4 us -> 86.1 us (0.963)
  blocking collectives: 53.5 us -> 67.6 us
  starting transfers between devices: 16.3 us -> 5.39 us
  waiting for transfers between devices: 14.3 us -> 6.86 us
    all_to_all x3, blocking collectives: 53.5 us -> 67.6 us  [exchange(): return lax.all_to_all(value, axes, 0, 0, tiled=True)]
    all_to_all x2 -> x1, starting transfers between devices: 16.3 us -> 5.39 us  [exchange(): return lax.all_to_all(value, axes, 0, 0, tiled=True)]
    all_to_all x2 -> x1, waiting for transfers between devices: 14.3 us -> 6.86 us  [exchange(): return lax.all_to_all(value, axes, 0, 0, tiled=True)]
    pallas_call x4 -> x5, Pallas kernels: 2.06 us -> 2.16 us  [the longest x1 0.96 us: stages(): call(contact_kernel, [((NGX, 8, 256), f32), ((2, ROWS, COLS), f32)], 'ssv...]
  transfers between devices with their start and end apart: 2 -> 1, of which waited for: 2 -> 1; matrix products, arithmetic and copies ran while one was open for 0% -> 0% of each run, Pallas kernels for 0% -> 0%
where the time goes in v3:
time: 86.1 us; the launch traced here: 85.7 us
  blocking collectives  67.6 us (79%)
  waiting for transfers between devices  6.86 us (8%)
  starting transfers between devices  5.39 us (6%)
  Pallas kernels  2.92 us (3%)
  between operations  2.04 us (2%)
    all_to_all x3, blocking collectives, exchange(): return lax.all_to_all(value, axes, 0, 0, tiled=True)  67.6 us
    all_to_all x1, waiting for transfers between devices, exchange(): return lax.all_to_all(value, axes, 0, 0, tiled=True)  6.86 us
    all_to_all x1, starting transfers between devices, exchange(): return lax.all_to_all(value, axes, 0, 0, tiled=True)  5.39 us
  transfers between devices with their start and end apart: 1, of which 1 were waited for; matrix products, arithmetic and copies ran while one was open for 0% of the time, Pallas kernels for 0%

profile of v3, /device:TPU:1, one launch (start us, length us, event | category | flops | bytes accessed | tf_op | source)
XLA Modules:
  0.0 85.7 jit_solution(9445241376449983792)
XLA Ops:
  1.3 0.0 copy-start
  1.3 0.0 copy-start.1
  1.3 0.0 copy-start.2
  1.4 0.8 copy-done
  2.1 0.0 copy-done.1
  2.1 0.0 copy-done.2
  2.1 0.1 shard_map.131
  2.3 39.7 %all_to_all.24.recv = bf16[16,3,4,128]{3,2,1,0:T(4,128)(2,1)S(1)} all-to-all(bf16[16,3,4,128]{3,2,1,0:T(4,128)(2,1)S(1)} %shard_map.131), channel_id=1, replica_groups=mesh['gx_0'=4,'gx_1'=4,'gx_2'=2,'gy'=16] {'gy'}, dimensions={0} | all-to-all | bytes 98304 | tf_op jit(solution)/shard_map/all_to_all | solution.py:392
  41.9 0.7 shard_map.132
  42.6 0.0 copy-start.5
  42.6 5.4 %all-to-all-start.2 = ((bf16[32,16,128]{2,1,0:T(8,128)(2,1)}), bf16[32,16,128]{2,1,0:T(8,128)(2,1)S(1)}, u32[]{:S(2)}, u32[]{:S(2)}) async-start(bf16[32,16,128]{2,1,0:T(8,128)(2,1)} %get-tuple-element.16), calls=%async_computation.2 | async-start | bytes 262144 | tf_op jit(solution)/shard_map/all_to_all | solution.py:392
  48.7 0.0 copy-done.5
  48.7 0.0 copy-start.6
  48.7 0.0 copy-start.7
  48.7 0.2 shard_map.133.slaves
  49.0 6.9 %all-to-all-done.2.recv = bf16[32,16,128]{2,1,0:T(8,128)(2,1)S(1)} async-done(((bf16[32,16,128]{2,1,0:T(8,128)(2,1)}), bf16[32,16,128]{2,1,0:T(8,128)(2,1)S(1)}, u32[]{:S(2)}, u32[]{:S(2)}) %all-to-all-start.2) | async-done | bytes 131104 | tf_op jit(solution)/shard_map/all_to_all | solution.py:392
  55.8 0.0 copy-done.6
  55.8 0.0 copy-done.7
  55.8 1.0 %shard_map.134 = (f32[32,8,256]{2,1,0:T(8,128)S(1)}, f32[2,32,256]{2,1,0:T(8,128)S(1)}) custom-call(s32[1]{0:T(128)} %copy.24.ids, s32[1]{0:T(128)S(6)} %copy.25.count, bf16[32,16,128]{2,1,0:T(8,128)(2,1)S(1)} %all-to-all-done.2.recv, f32[8,128]{1,0:T(8,128)S(1)} %get-tuple-element.17.sides, f32[2,1024]{1,0:T(2,128)S(1)} %shard_map.133.slaves, ...), custom_call_target="tpu_custom_call" | custom-call | flops 1000000 | bytes 1048576 | tf_op jit(solution)/shard_map/pallas_call | solution.py:429
  56.8 13.3 %all_to_all.25.recv = f32[32,8,256]{2,1,0:T(8,128)S(1)} all-to-all(f32[32,8,256]{2,1,0:T(8,128)S(1)} %get-tuple-element.18), channel_id=1, replica_groups=mesh['gx_0'=4,'gx_1'=4,'gx_2'=2,'gy'=16] {'gx_0','gx_1','gx_2'}, dimensions={0} | all-to-all | bytes 524288 | tf_op jit(solution)/shard_map/all_to_all | solution.py:392
  70.1 0.0 copy-start.3
  70.1 0.2 shard_map.135
  70.3 0.0 copy-start.4
  70.3 14.6 %all_to_all.26.recv = f32[16,2,128]{2,1,0:T(2,128)S(1)} all-to-all(f32[16,2,128]{2,1,0:T(2,128)S(1)} %shard_map.135), channel_id=1, replica_groups=mesh['gx_0'=4,'gx_1'=4,'gx_2'=2,'gy'=16] {'gy'}, dimensions={0} | all-to-all | bytes 32768 | tf_op jit(solution)/shard_map/all_to_all | solution.py:392
  84.9 0.0 copy-done.3
  84.9 0.0 copy-done.4
  84.9 0.8 shard_map.136
  (2 shorter events, 0.0 us)
Async XLA Ops:
  1.3 0.8 copy-start
  1.3 0.8 copy-start.1
  1.3 0.8 copy-start.2
  42.6 6.1 %copy-start.5 = (s32[1,1024]{1,0:T(1,128)S(1)}, s32[1,1024]{1,0:T(1,128)}, u32[]{:S(2)}) copy-start(s32[1,1024]{1,0:T(1,128)} %pair_node.3) | copy-start | bytes 12292
  42.6 13.2 %all-to-all-start.2 = ((bf16[32,16,128]{2,1,0:T(8,128)(2,1)}), bf16[32,16,128]{2,1,0:T(8,128)(2,1)S(1)}, u32[]{:S(2)}, u32[]{:S(2)}) async-start(bf16[32,16,128]{2,1,0:T(8,128)(2,1)} %get-tuple-element.16), calls=%async_computation.2 | async-start | bytes 262144 | tf_op jit(solution)/shard_map/all_to_all | solution.py:392
  48.7 7.1 %copy-start.6 = (s32[1,1024]{1,0:T(1,128)S(1)}, s32[1,1024]{1,0:T(1,128)}, u32[]{:S(2)}) copy-start(s32[1,1024]{1,0:T(1,128)} %pair_segment.1) | copy-start | bytes 12292
  48.7 7.1 %copy-start.7 = (s32[1,1024]{1,0:T(1,128)S(1)}, s32[1,1024]{1,0:T(1,128)}, u32[]{:S(2)}) copy-start(s32[1,1024]{1,0:T(1,128)} %pair_side.1) | copy-start | bytes 12292
  70.1 14.8 %copy-start.3 = (f32[2,32,256]{2,1,0:T(8,128)S(1)}, f32[2,32,256]{2,1,0:T(8,128)}, u32[]{:S(2)}) copy-start(f32[2,32,256]{2,1,0:T(8,128)} %vel.1) | copy-start | bytes 196612
  70.3 14.6 %copy-start.4 = (f32[32,256]{1,0:T(8,128)S(1)}, f32[32,256]{1,0:T(8,128)}, u32[]{:S(2)}) copy-start(f32[32,256]{1,0:T(8,128)} %mass.7) | copy-start | bytes 98308

commit v4 on v3

--- a/solution.py
+++ b/solution.py
@@ -17,7 +17,6 @@
 TOTAL_COLS = NGY * COLS
 STIFFNESS = 10.0
 GAP_SCALE = 0.05
-BLOCK = 256
 
 f32 = jnp.float32
 bf16 = jnp.bfloat16
@@ -49,14 +48,7 @@
     return jnp.sum(out, axis=0, keepdims=True)
 
 
-def spread_kernel(ids, chunk, disp, energy, mass, out):
-    _, _, gy = place(ids)
-    for h in range(2):
-        rows = [chunk[2 * r + h, c : c + 1].astype(f32) for c in range(2) for r in range(2)]
-        coords = rows_of(rows)[0:4].astype(bf16)
-        for z in range(NGY):
-            out[z, h] = coords
-
+def edges(gy, disp, energy, mass, out):
     def edge(at):
         cut = slice(at, at + 1)
         columns = [disp[0, :, cut], disp[1, :, cut], energy[:, cut] * mass[:, cut]]
@@ -66,6 +58,28 @@
     for z in range(NGY):
         out[z, 2] = head
     out[lax.rem(gy + 1, NGY), 2] = tail
+
+
+def spread_kernel(ids, count, recv, disp, energy, mass, out, extra):
+    owner, _, gy = place(ids)
+    chunk = recv[owner // NGY].astype(f32)
+    for h in range(2):
+        rows = [chunk[2 * r + h, c : c + 1] for c in range(2) for r in range(2)]
+        coords = rows_of(rows)[0:4].astype(bf16)
+        for z in range(NGY):
+            out[z, h] = coords
+    extra[0:8] = rows_of([chunk[r, 2 + c : 3 + c] for c in range(2) for r in range(4)])
+    extra[8:16] = jnp.full((8, 128), count[0].astype(f32))
+    edges(gy, disp, energy, mass, out)
+
+
+def idle_kernel(ids, count, disp, energy, mass, out, extra):
+    _, _, gy = place(ids)
+    for z in range(NGY):
+        out[z] = jnp.zeros((3, 4, 128), bf16)
+    extra[0:8] = jnp.zeros((8, 128), f32)
+    extra[8:16] = jnp.full((8, 128), count[0].astype(f32))
+    edges(gy, disp, energy, mass, out)
 
 
 def gather_kernel(ids, recv, disp, energy, mass, out, sides):
@@ -198,21 +212,12 @@
     return jnp.where(at == index.astype(f32).astype(bf16), jnp.ones((), bf16), jnp.zeros((), bf16))
 
 
-def blocks_of(live_count):
-    return (live_count + BLOCK - 1) // BLOCK
-
-
-def block_at(index):
-    begin = pl.multiple_of(index * BLOCK, BLOCK)
-    return begin, (slice(None), pl.ds(begin, BLOCK))
-
-
 def node_place(node):
     row = ((node >> 7) & 1) * 32 + (node >> 8)
-    return one_hot(128, node & 127), iota((64, BLOCK), 0) == row
-
-
-def slave_kernel(count, disp, pair_node, out, nodes):
+    return one_hot(128, node & 127), iota((64, PAIRS), 0) == row
+
+
+def slave_places(disp, pair_node, nodes):
     for c in range(2):
         for h in range(2):
             rest = disp[c, :, 128 * h : 128 * h + 128]
@@ -221,26 +226,21 @@
                 at = 128 * k + 64 * c + 32 * h
                 nodes[at : at + 32] = high.astype(bf16)
                 rest = low
-
-    def block(index, carry):
-        _, cut = block_at(index)
-        lanes, mask = node_place(pair_node[cut])
-        seen = jnp.dot(nodes[...], lanes, preferred_element_type=f32)
-        seen = (seen[256:384] + seen[128:256]) + seen[0:128]
-        for c in range(2):
-            found = jnp.where(mask, seen[64 * c : 64 * c + 64], 0.0)
-            out[c : c + 1, cut[1]] = jnp.sum(found, axis=0, keepdims=True)
-        return carry
-
-    lax.fori_loop(0, blocks_of(count[0]), block, 0)
+    lanes, mask = node_place(pair_node[...])
+    seen = jnp.dot(nodes[...], lanes, preferred_element_type=f32)
+    seen = (seen[256:384] + seen[128:256]) + seen[0:128]
+    found = [
+        jnp.sum(jnp.where(mask, seen[64 * c : 64 * c + 64], 0.0), axis=0, keepdims=True)
+        for c in range(2)
+    ]
+    return found, lanes, mask
 
 
 def contact_kernel(
     ids,
-    count,
+    extra,
     recv,
     sides,
-    slaves,
     disp,
     energy,
     mass,
@@ -251,78 +251,68 @@
     force,
     field,
     coords,
+    nodes,
     picks,
-    reaction,
-    pushed,
 ):
+    slave, node_lanes, node_mask = slave_places(disp, pair_node, nodes)
+    row8 = iota((8, 128), 0)
+    for i in range(NGX // 4):
+        left, right = [], []
+        for s in (4 * i, 4 * i + 2):
+            even, odd = recv[s, 0:8].astype(f32), recv[s + 1, 0:8].astype(f32)
+            left.append(jnp.where(row8 < 4, even, pltpu.roll(odd, 4, 0)))
+            right.append(jnp.where(row8 < 4, pltpu.roll(even, 4, 0), odd))
+        coords[16 * i : 16 * i + 16, 0:128] = jnp.concatenate(left, axis=0).astype(bf16)
+        coords[16 * i : 16 * i + 16, 128:256] = jnp.concatenate(right, axis=0).astype(bf16)
+
+    segment = pair_segment[...]
+    ends = jnp.concatenate([segment, segment + 1], axis=1)
+    lanes = one_hot(256, ends & 255)
+    piece, line = ends >> 9, (ends >> 8) & 1
+    looked = jnp.dot(coords[...], lanes, preferred_element_type=f32)
+    found = jnp.zeros((8, 2 * PAIRS), f32)
+    for s in range(NGX // 2):
+        found = found + jnp.where((piece >> 1) == s, looked[8 * s : 8 * s + 8], 0.0)
+    row = iota((8, 2 * PAIRS), 0)
+    at = (piece & 1) * 4 + line
+    end_x = jnp.sum(jnp.where(row == at, found, 0.0), axis=0, keepdims=True)
+    end_y = jnp.sum(jnp.where(row == at + 2, found, 0.0), axis=0, keepdims=True)
+
+    live = iota((1, PAIRS), 1).astype(f32) < extra[8:9, 0:1]
+    push_x, push_y, magnitude, fraction = contact_terms(
+        slave[0],
+        slave[1],
+        end_x[:, :PAIRS],
+        end_y[:, :PAIRS],
+        end_x[:, PAIRS:],
+        end_y[:, PAIRS:],
+        pair_side[...],
+        live,
+    )
+    share = jnp.concatenate([1.0 - fraction, fraction], axis=1)
+    terms = [share * jnp.concatenate([v, v], axis=1) for v in (-push_x, -push_y, magnitude)]
+    stacked = jnp.where(row < 2, terms[0], jnp.where(row < 4, terms[1], terms[2]))
+    stacked = jnp.where((row < 6) & ((row & 1) == line), stacked, 0.0)
+    high, low = high_low(stacked)
+    high = jnp.concatenate([high, high], axis=0).astype(bf16)
+    low = jnp.concatenate([low, low], axis=0).astype(bf16)
+    half = iota((16, 2 * PAIRS), 0) >> 3
+    offset = (piece - half).astype(f32).astype(bf16)
+    nothing = jnp.zeros((), bf16)
+    for s in range(NGX // 2):
+        mine = offset == jnp.asarray(2 * s, bf16)
+        picks[16 * s : 16 * s + 16] = jnp.where(mine, high, nothing)
+        picks[256 + 16 * s : 272 + 16 * s] = jnp.where(mine, low, nothing)
+    contract = (((1,), (1,)), ((), ()))
+    part = lax.dot_general(picks[...], lanes, contract, preferred_element_type=f32)
+    reaction = part[0:256] + part[256:512]
+
+    rows = [jnp.where(node_mask, half, 0.0) for v in (push_x, push_y) for half in high_low(v)]
+    rows = jnp.concatenate([rows[0], rows[2], rows[1], rows[3]], axis=0).astype(bf16)
+    part = lax.dot_general(rows, node_lanes, contract, preferred_element_type=f32)
+    pushed = part[0:128] + part[128:256]
+
     least = zone_forces(ids, recv, sides, disp, energy, mass, field, force)
-    row8 = iota((8, 128), 0)
-    for i in range(NGX // 2):
-        even, odd = recv[2 * i, 0:8].astype(f32), recv[2 * i + 1, 0:8].astype(f32)
-        field[0, 8 * (i % 4) : 8 * (i % 4) + 8, 0:128] = jnp.where(row8 < 4, even, pltpu.roll(odd, 4, 0))
-        field[0, 8 * (i % 4) : 8 * (i % 4) + 8, 128:256] = jnp.where(row8 < 4, pltpu.roll(even, 4, 0), odd)
-        if i % 4 == 3:
-            coords[8 * i - 24 : 8 * i + 8] = field[0, 0:32, 0:256].astype(bf16)
-    reaction[...] = jnp.zeros_like(reaction)
-    pushed[...] = jnp.zeros_like(pushed)
-    live_count = count[0]
-
-    def block(index, carry):
-        begin, cut = block_at(index)
-        segment = pair_segment[cut]
-        ends = jnp.concatenate([segment, segment + 1], axis=1)
-        lanes = one_hot(256, ends & 255)
-        piece, line = ends >> 9, (ends >> 8) & 1
-        looked = jnp.dot(coords[...], lanes, preferred_element_type=f32)
-        found = jnp.zeros((8, 2 * BLOCK), f32)
-        for s in range(NGX // 2):
-            found = found + jnp.where((piece >> 1) == s, looked[8 * s : 8 * s + 8], 0.0)
-        row = iota((8, 2 * BLOCK), 0)
-        at = (piece & 1) * 4 + line
-        end_x = jnp.sum(jnp.where(row == at, found, 0.0), axis=0, keepdims=True)
-        end_y = jnp.sum(jnp.where(row == at + 2, found, 0.0), axis=0, keepdims=True)
-
-        live = begin + iota((1, BLOCK), 1) < live_count
-        push_x, push_y, magnitude, fraction = contact_terms(
-            slaves[0:1, cut[1]],
-            slaves[1:2, cut[1]],
-            end_x[:, :BLOCK],
-            end_y[:, :BLOCK],
-            end_x[:, BLOCK:],
-            end_y[:, BLOCK:],
-            pair_side[cut],
-            live,
-        )
-        push_x, push_y = jnp.where(live, push_x, 0.0), jnp.where(live, push_y, 0.0)
-        fraction = jnp.where(live, fraction, 0.0)
-        share = jnp.concatenate([1.0 - fraction, fraction], axis=1)
-        terms = [
-            share * jnp.concatenate([v, v], axis=1) for v in (-push_x, -push_y, magnitude)
-        ]
-        stacked = jnp.where(row < 2, terms[0], jnp.where(row < 4, terms[1], terms[2]))
-        stacked = jnp.where((row < 6) & ((row & 1) == line), stacked, 0.0)
-        high, low = high_low(stacked)
-        high = jnp.concatenate([high, high], axis=0).astype(bf16)
-        low = jnp.concatenate([low, low], axis=0).astype(bf16)
-        half = iota((16, 2 * BLOCK), 0) >> 3
-        offset = (piece - half).astype(f32).astype(bf16)
-        nothing = jnp.zeros((), bf16)
-        for s in range(NGX // 2):
-            mine = offset == jnp.asarray(2 * s, bf16)
-            picks[16 * s : 16 * s + 16] = jnp.where(mine, high, nothing)
-            picks[256 + 16 * s : 272 + 16 * s] = jnp.where(mine, low, nothing)
-        contract = (((1,), (1,)), ((), ()))
-        part = lax.dot_general(picks[...], lanes, contract, preferred_element_type=f32)
-        reaction[...] += part[0:256] + part[256:512]
-
-        lanes, mask = node_place(pair_node[cut])
-        rows = [jnp.where(mask, half, 0.0) for v in (push_x, push_y) for half in high_low(v)]
-        rows = jnp.concatenate([rows[0], rows[2], rows[1], rows[3]], axis=0).astype(bf16)
-        part = lax.dot_general(rows, lanes, contract, preferred_element_type=f32)
-        pushed[...] += part[0:128] + part[128:256]
-        return carry
-
-    lax.fori_loop(0, blocks_of(live_count), block, 0)
     for c in range(2):
         for h in range(2):
             at = 64 * c + 32 * h
@@ -332,7 +322,7 @@
         out[s] = jnp.where(row == 6, least, reaction[8 * s : 8 * s + 8])
 
 
-def sum_kernel(recv, chunk, out):
+def sum_kernel(recv, extra, out):
     total = recv[0]
     least = recv[0]
     for s in range(1, NGX):
@@ -351,7 +341,7 @@
             row = rows[2 * c + z // 8 : 2 * c + z // 8 + 1]
             line = jnp.where(mine, pltpu.roll(row, shift, 1) if shift else row, line)
             if c < 2:
-                row = chunk[z // 4, 2 + c : 3 + c].astype(f32)
+                row = extra[4 * c + z // 4 : 4 * c + z // 4 + 1]
                 old = jnp.where(mine, pltpu.roll(row, shift, 1) if shift else row, old)
         out[z, 0:1] = line
         out[z, 1:2] = old
@@ -392,13 +382,18 @@
     return lax.all_to_all(value, axes, 0, 0, tiled=True)
 
 
-def owner_piece(exchange, master_block, owner):
-    def send():
-        tiles = master_block[0].reshape(4, NGX, 4, 128).transpose(1, 2, 0, 3)
-        return lax.dynamic_index_in_dim(exchange(tiles, GX), owner[0] // NGY, 0, False)
+def owner_piece(exchange, master_block, owner, count, fields):
+    tiles = master_block[0].reshape(4, NGX, 4, 128).transpose(1, 2, 0, 3)
+    out = [((NGY, 3, 4, 128), bf16), ((16, 128), f32)]
+
+    def send(tiles, owner, count, *fields):
+        return tuple(call(spread_kernel, out, "ssvvvv")(owner, count, exchange(tiles, GX), *fields))
+
+    def idle(tiles, owner, count, *fields):
+        return tuple(call(idle_kernel, out, "ssvvv")(owner, count, *fields))
 
     mine = lax.axis_index("gy") == lax.rem(owner[0], NGY)
-    return lax.cond(mine, send, lambda: jnp.zeros((4, 4, 128), bf16))
+    return lax.cond(mine, send, idle, tiles, owner, count, *fields)
 
 
 def stages(
@@ -416,30 +411,25 @@
     pair_count,
 ):
     fields = (node_disp, zone_energy, zone_mass)
-    chunk = owner_piece(exchange, master_block, owner)
-    (sent,) = call(spread_kernel, [((NGY, 3, 4, 128), bf16)], "svvvv")(owner, chunk, *fields)
+    sent, extra = owner_piece(exchange, master_block, owner, pair_count, fields)
     sent = exchange(sent, "gy")
     sent, sides = call(gather_kernel, [((NGX, 16, 128), bf16), ((8, 128), f32)], "svvvv")(
         owner, sent, *fields
     )
-    (slaves,) = call(
-        slave_kernel, [((2, PAIRS), f32)], "svv", [((384, 128), bf16)], flops=100_000_000
-    )(pair_count, node_disp, pair_node)
     sent = exchange(sent, GX)
     sent, force = call(
         contact_kernel,
         [((NGX, 8, 256), f32), ((2, ROWS, COLS), f32)],
-        "ssvvvvvvvvv",
+        "svvvvvvvvv",
         [
             ((3, ROWS + 8, COLS + 128), f32),
             ((128, 256), bf16),
-            ((512, 2 * BLOCK), bf16),
-            ((256, 256), f32),
-            ((128, 128), f32),
+            ((384, 128), bf16),
+            ((512, 2 * PAIRS), bf16),
         ],
-    )(owner, pair_count, sent, sides, slaves, *fields, pair_node, pair_segment, pair_side)
+    )(owner, extra, sent, sides, *fields, pair_node, pair_segment, pair_side)
     sent = exchange(sent, GX)
-    (sent,) = call(sum_kernel, [((NGY, 2, 128), f32)], "vv")(sent, chunk)
+    (sent,) = call(sum_kernel, [((NGY, 2, 128), f32)], "vv")(sent, extra)
     sent = exchange(sent, "gy")
     return tuple(
         call(

time: 86.1 us -> 83.2 us (0.966)
  blocking collectives: 67.6 us -> 75.8 us
  waiting for transfers between devices: 6.86 us -> 0 us
  starting transfers between devices: 5.39 us -> 0 us
  Pallas kernels: 2.92 us -> 4.85 us
    all_to_all x3 -> x4, blocking collectives: 67.6 us -> 75.8 us  [exchange(): return lax.all_to_all(value, axes, 0, 0, tiled=True)]
    all_to_all x1 -> x0, waiting for transfers between devices: 6.86 us -> none  [exchange(): return lax.all_to_all(value, axes, 0, 0, tiled=True)]
    all_to_all x1 -> x0, starting transfers between devices: 5.39 us -> none  [exchange(): return lax.all_to_all(value, axes, 0, 0, tiled=True)]
    pallas_call x4 -> x3, Pallas kernels: 1.48 us -> 4.07 us  [the longest x1 2.24 us: idle(): return tuple(call(idle_kernel, out, 'ssvvv')(owner, count, *fields))]
  transfers between devices with their start and end apart: 1 -> 0, of which waited for: 1 -> 0; matrix products, arithmetic and copies ran while one was open for 0% -> 0% of each run, Pallas kernels for 0% -> 0%
where the time goes in v4:
time: 83.2 us; the launch traced here: 82.2 us
  blocking collectives  75.8 us (91%)
  Pallas kernels  4.85 us (6%)
  between operations  1.39 us (2%)
    all_to_all x4, blocking collectives, exchange(): return lax.all_to_all(value, axes, 0, 0, tiled=True)  75.8 us
    pallas_call x1, Pallas kernels, idle(): return tuple(call(idle_kernel, out, 'ssvvv')(owner, count, *fields))  2.24 us

profile of v4, /device:TPU:1, one launch (start us, length us, event | category | flops | bytes accessed | tf_op | source)
XLA Modules:
  0.0 82.2 jit_solution(7558106402253716356)
XLA Ops:
  0.6 0.0 copy-start.7
  1.3 0.1 copy-done.7
  1.4 2.2 %conditional.1 = ((bf16[16,3,4,128]{3,2,1,0:T(4,128)(2,1)S(1)}, f32[16,128]{1,0:T(8,128)S(1)})) conditional(s32[]{:T(128)} %convert_element_type.3, (s32[1]{0:T(128)}, s32[1]{0:T(128)}, f32[2,32,256]{2,1,0:T(8,128)}, f32[32,256]{1,0:T(8,128)S(1)}, f32[32,256]{1,0:T(8,128)}) %tuple.19, (bf16[32,4,4,128]{3,2,1,0:T(4,128)(2,1)}, s32[1]{0:T(128)}, ...), branch_computations={%region_0.0_spmd, %region_1.0_spmd} | conditional | flops 1000000 | bytes 1704000 | solution.py:396
  1.4 2.2 %branch_0_fun.1 = (bf16[16,3,4,128]{3,2,1,0:T(4,128)(2,1)S(1)}, f32[16,128]{1,0:T(8,128)S(1)}) custom-call(s32[1]{0:T(128)} %get-tuple-element.22.ids, s32[1]{0:T(128)} %get-tuple-element.23.count, f32[2,32,256]{2,1,0:T(8,128)} %get-tuple-element.24.disp, f32[32,256]{1,0:T(8,128)S(1)} %get-tuple-element.25.energy, f32[32,256]{1,0:T(8,128)} %get-tuple-element.26.mass), custom_call_target="tpu_custom_call" | custom-call | flops 1000000 | bytes 1048576 | tf_op jit(solution)/shard_map/cond/branch_0_fun/pallas_call | solution.py:393
  3.6 0.0 copy-start.5
  3.7 0.0 copy-start.8
  3.7 36.7 %all_to_all.25.recv = bf16[16,3,4,128]{3,2,1,0:T(4,128)(2,1)S(1)} all-to-all(bf16[16,3,4,128]{3,2,1,0:T(4,128)(2,1)S(1)} %get-tuple-element.43), channel_id=1, replica_groups=mesh['gx_0'=4,'gx_1'=4,'gx_2'=2,'gy'=16] {'gy'}, dimensions={0} | all-to-all | bytes 98304 | tf_op jit(solution)/shard_map/all_to_all | solution.py:382
  40.3 0.0 copy-done.5
  40.3 0.0 copy-done.8
  40.4 0.0 copy-start.2
  40.4 0.0 copy-start.3
  40.4 0.0 copy-start.4
  40.4 12.8 %all_to_all.26.recv = bf16[32,16,128]{2,1,0:T(8,128)(2,1)S(1)} all-to-all(bf16[32,16,128]{2,1,0:T(8,128)(2,1)S(1)} %get-tuple-element.44), channel_id=1, replica_groups=mesh['gx_0'=4,'gx_1'=4,'gx_2'=2,'gy'=16] {'gx_0','gx_1','gx_2'}, dimensions={0} | all-to-all | bytes 262144 | tf_op jit(solution)/shard_map/all_to_all | solution.py:382
  53.2 0.0 copy-done.2
  53.2 0.0 copy-done.3
  53.2 0.0 copy-done.4
  53.2 1.6 %shard_map.131 = (f32[32,8,256]{2,1,0:T(8,128)S(1)}, f32[2,32,256]{2,1,0:T(8,128)S(1)}) custom-call(s32[1]{0:T(128)} %copy.18.ids, f32[16,128]{1,0:T(8,128)S(1)} %get-tuple-element.42.extra, bf16[32,16,128]{2,1,0:T(8,128)(2,1)S(1)} %all_to_all.26.recv, f32[8,128]{1,0:T(8,128)S(1)} %get-tuple-element.45.sides, f32[2,32,256]{2,1,0:T(8,128)S(1)} %copy-done.5, ...), custom_call_target="tpu_custom_call" | custom-call | flops 1000000 | bytes 1048576 | tf_op jit(solution)/shard_map/pallas_call | solution.py:420
  54.9 12.5 %all_to_all.27.recv = f32[32,8,256]{2,1,0:T(8,128)S(1)} all-to-all(f32[32,8,256]{2,1,0:T(8,128)S(1)} %get-tuple-element.46), channel_id=1, replica_groups=mesh['gx_0'=4,'gx_1'=4,'gx_2'=2,'gy'=16] {'gx_0','gx_1','gx_2'}, dimensions={0} | all-to-all | bytes 524288 | tf_op jit(solution)/shard_map/all_to_all | solution.py:382
  67.4 0.0 copy-start
  67.4 0.2 shard_map.132
  67.6 0.0 copy-start.1
  67.6 13.8 %all_to_all.28.recv = f32[16,2,128]{2,1,0:T(2,128)S(1)} all-to-all(f32[16,2,128]{2,1,0:T(2,128)S(1)} %shard_map.132), channel_id=1, replica_groups=mesh['gx_0'=4,'gx_1'=4,'gx_2'=2,'gy'=16] {'gy'}, dimensions={0} | all-to-all | bytes 32768 | tf_op jit(solution)/shard_map/all_to_all | solution.py:382
  81.4 0.0 copy-done
  81.4 0.0 copy-done.1
  81.4 0.8 shard_map.133
  (1 shorter events, 0.0 us)
Async XLA Ops:
  0.6 0.8 copy-start.7
  3.6 36.7 %copy-start.5 = (f32[2,32,256]{2,1,0:T(8,128)S(1)}, f32[2,32,256]{2,1,0:T(8,128)}, u32[]{:S(2)}) copy-start(f32[2,32,256]{2,1,0:T(8,128)} %disp.5) | copy-start | bytes 196612
  3.7 36.7 %copy-start.8 = (f32[32,256]{1,0:T(8,128)S(1)}, f32[32,256]{1,0:T(8,128)}, u32[]{:S(2)}) copy-start(f32[32,256]{1,0:T(8,128)} %mass.4) | copy-start | bytes 98308
  40.4 12.8 %copy-start.2 = (s32[1,1024]{1,0:T(1,128)S(1)}, s32[1,1024]{1,0:T(1,128)}, u32[]{:S(2)}) copy-start(s32[1,1024]{1,0:T(1,128)} %pair_node.1) | copy-start | bytes 12292
  40.4 12.8 %copy-start.3 = (s32[1,1024]{1,0:T(1,128)S(1)}, s32[1,1024]{1,0:T(1,128)}, u32[]{:S(2)}) copy-start(s32[1,1024]{1,0:T(1,128)} %pair_segment.1) | copy-start | bytes 12292
  40.4 12.8 %copy-start.4 = (s32[1,1024]{1,0:T(1,128)S(1)}, s32[1,1024]{1,0:T(1,128)}, u32[]{:S(2)}) copy-start(s32[1,1024]{1,0:T(1,128)} %pair_side.1) | copy-start | bytes 12292
  67.4 14.0 %copy-start = (f32[2,32,256]{2,1,0:T(8,128)S(1)}, f32[2,32,256]{2,1,0:T(8,128)}, u32[]{:S(2)}) copy-start(f32[2,32,256]{2,1,0:T(8,128)} %vel.1) | copy-start | bytes 196612
  67.6 13.8 %copy-start.1 = (f32[32,256]{1,0:T(8,128)S(1)}, f32[32,256]{1,0:T(8,128)}, u32[]{:S(2)}) copy-start(f32[32,256]{1,0:T(8,128)} %mass.5) | copy-start | bytes 98308

commit v5 on v4

--- a/solution.py
+++ b/solution.py
@@ -48,7 +48,27 @@
     return jnp.sum(out, axis=0, keepdims=True)
 
 
-def edges(gy, disp, energy, mass, out):
+def count_tile(count):
+    return jnp.full((8, 128), count[0].astype(f32))
+
+
+def pick_kernel(owner, count, recv, chunk, tile):
+    chunk[...] = recv[owner[0] // NGY]
+    tile[...] = count_tile(count)
+
+
+def idle_kernel(count, chunk, tile):
+    chunk[...] = jnp.zeros((4, 4, 128), bf16)
+    tile[...] = count_tile(count)
+
+
+def spread_kernel(chunk, disp, energy, mass, out):
+    for h in range(2):
+        rows = [chunk[2 * r + h, c : c + 1].astype(f32) for c in range(2) for r in range(2)]
+        coords = rows_of(rows)[0:4].astype(bf16)
+        for z in range(NGY):
+            out[z, h] = coords
+
     def edge(at):
         cut = slice(at, at + 1)
         columns = [disp[0, :, cut], disp[1, :, cut], energy[:, cut] * mass[:, cut]]
@@ -57,29 +77,7 @@
     head, tail = edge(0), edge(COLS - 1)
     for z in range(NGY):
         out[z, 2] = head
-    out[lax.rem(gy + 1, NGY), 2] = tail
-
-
-def spread_kernel(ids, count, recv, disp, energy, mass, out, extra):
-    owner, _, gy = place(ids)
-    chunk = recv[owner // NGY].astype(f32)
-    for h in range(2):
-        rows = [chunk[2 * r + h, c : c + 1] for c in range(2) for r in range(2)]
-        coords = rows_of(rows)[0:4].astype(bf16)
-        for z in range(NGY):
-            out[z, h] = coords
-    extra[0:8] = rows_of([chunk[r, 2 + c : 3 + c] for c in range(2) for r in range(4)])
-    extra[8:16] = jnp.full((8, 128), count[0].astype(f32))
-    edges(gy, disp, energy, mass, out)
-
-
-def idle_kernel(ids, count, disp, energy, mass, out, extra):
-    _, _, gy = place(ids)
-    for z in range(NGY):
-        out[z] = jnp.zeros((3, 4, 128), bf16)
-    extra[0:8] = jnp.zeros((8, 128), f32)
-    extra[8:16] = jnp.full((8, 128), count[0].astype(f32))
-    edges(gy, disp, energy, mass, out)
+    out[lax.rem(lax.axis_index("gy") + 1, NGY), 2] = tail
 
 
 def gather_kernel(ids, recv, disp, energy, mass, out, sides):
@@ -238,7 +236,7 @@
 
 def contact_kernel(
     ids,
-    extra,
+    count,
     recv,
     sides,
     disp,
@@ -278,7 +276,7 @@
     end_x = jnp.sum(jnp.where(row == at, found, 0.0), axis=0, keepdims=True)
     end_y = jnp.sum(jnp.where(row == at + 2, found, 0.0), axis=0, keepdims=True)
 
-    live = iota((1, PAIRS), 1).astype(f32) < extra[8:9, 0:1]
+    live = iota((1, PAIRS), 1).astype(f32) < count[0:1, 0:1]
     push_x, push_y, magnitude, fraction = contact_terms(
         slave[0],
         slave[1],
@@ -322,7 +320,7 @@
         out[s] = jnp.where(row == 6, least, reaction[8 * s : 8 * s + 8])
 
 
-def sum_kernel(recv, extra, out):
+def sum_kernel(recv, chunk, out):
     total = recv[0]
     least = recv[0]
     for s in range(1, NGX):
@@ -341,7 +339,7 @@
             row = rows[2 * c + z // 8 : 2 * c + z // 8 + 1]
             line = jnp.where(mine, pltpu.roll(row, shift, 1) if shift else row, line)
             if c < 2:
-                row = extra[4 * c + z // 4 : 4 * c + z // 4 + 1]
+                row = chunk[z // 4, 2 + c : 3 + c].astype(f32)
                 old = jnp.where(mine, pltpu.roll(row, shift, 1) if shift else row, old)
         out[z, 0:1] = line
         out[z, 1:2] = old
@@ -382,18 +380,18 @@
     return lax.all_to_all(value, axes, 0, 0, tiled=True)
 
 
-def owner_piece(exchange, master_block, owner, count, fields):
+def owner_piece(exchange, master_block, owner, count):
     tiles = master_block[0].reshape(4, NGX, 4, 128).transpose(1, 2, 0, 3)
-    out = [((NGY, 3, 4, 128), bf16), ((16, 128), f32)]
-
-    def send(tiles, owner, count, *fields):
-        return tuple(call(spread_kernel, out, "ssvvvv")(owner, count, exchange(tiles, GX), *fields))
-
-    def idle(tiles, owner, count, *fields):
-        return tuple(call(idle_kernel, out, "ssvvv")(owner, count, *fields))
-
-    mine = lax.axis_index("gy") == lax.rem(owner[0], NGY)
-    return lax.cond(mine, send, idle, tiles, owner, count, *fields)
+    out = [((4, 4, 128), bf16), ((8, 128), f32)]
+
+    def send(tiles, owner, count):
+        return tuple(call(pick_kernel, out, "ssv")(owner, count, exchange(tiles, GX)))
+
+    def idle(tiles, owner, count):
+        return tuple(call(idle_kernel, out, "s")(count))
+
+    mine = lax.axis_index("gy") == (owner[0] & (NGY - 1))
+    return lax.cond(mine, send, idle, tiles, owner, count)
 
 
 def stages(
@@ -411,7 +409,8 @@
     pair_count,
 ):
     fields = (node_disp, zone_energy, zone_mass)
-    sent, extra = owner_piece(exchange, master_block, owner, pair_count, fields)
+    chunk, count = owner_piece(exchange, master_block, owner, pair_count)
+    (sent,) = call(spread_kernel, [((NGY, 3, 4, 128), bf16)], "vvvv")(chunk, *fields)
     sent = exchange(sent, "gy")
     sent, sides = call(gather_kernel, [((NGX, 16, 128), bf16), ((8, 128), f32)], "svvvv")(
         owner, sent, *fields
@@ -427,9 +426,9 @@
             ((384, 128), bf16),
             ((512, 2 * PAIRS), bf16),
         ],
-    )(owner, extra, sent, sides, *fields, pair_node, pair_segment, pair_side)
+    )(owner, count, sent, sides, *fields, pair_node, pair_segment, pair_side)
     sent = exchange(sent, GX)
-    (sent,) = call(sum_kernel, [((NGY, 2, 128), f32)], "vv")(sent, extra)
+    (sent,) = call(sum_kernel, [((NGY, 2, 128), f32)], "vv")(sent, chunk)
     sent = exchange(sent, "gy")
     return tuple(
         call(

time: 83.2 us -> 84.7 us (1.018)
  blocking collectives: 75.8 us -> 78.9 us
  Pallas kernels: 4.85 us -> 3.38 us
    all_to_all x4, blocking collectives: 75.8 us -> 78.9 us  [exchange(): return lax.all_to_all(value, axes, 0, 0, tiled=True)]
    pallas_call x2 -> x3, Pallas kernels: 2.42 us -> 0.95 us  [the longest x1 0.67 us: idle(): return tuple(call(idle_kernel, out, 's')(count))]
where the time goes in v5:
time: 84.7 us; the launch traced here: 83.9 us
  blocking collectives  78.9 us (93%)
  Pallas kernels  3.38 us (4%)
  between operations  1.38 us (2%)
    all_to_all x4, blocking collectives, exchange(): return lax.all_to_all(value, axes, 0, 0, tiled=True)  78.9 us

profile of v5, /device:TPU:1, one launch (start us, length us, event | category | flops | bytes accessed | tf_op | source)
XLA Modules:
  0.0 83.9 jit_solution(4971147718396988048)
XLA Ops:
  1.3 0.0 copy-start
  1.3 0.0 copy-start.1
  1.3 0.0 copy-start.2
  1.3 0.7 conditional.1
  1.3 0.7 branch_0_fun.1
  2.0 0.1 copy-done
  2.1 0.0 copy-done.1
  2.1 0.0 copy-done.2
  2.1 0.1 shard_map.133
  2.2 39.8 %all_to_all.25.recv = bf16[16,3,4,128]{3,2,1,0:T(4,128)(2,1)S(1)} all-to-all(bf16[16,3,4,128]{3,2,1,0:T(4,128)(2,1)S(1)} %shard_map.133), channel_id=1, replica_groups=mesh['gx_0'=4,'gx_1'=4,'gx_2'=2,'gy'=16] {'gy'}, dimensions={0} | all-to-all | bytes 98304 | tf_op jit(solution)/shard_map/all_to_all | solution.py:380
  42.1 0.0 copy-start.5
  42.1 0.0 copy-start.6
  42.1 0.0 copy-start.7
  42.1 12.8 %all_to_all.26.recv = bf16[32,16,128]{2,1,0:T(8,128)(2,1)S(1)} all-to-all(bf16[32,16,128]{2,1,0:T(8,128)(2,1)S(1)} %get-tuple-element.21), channel_id=1, replica_groups=mesh['gx_0'=4,'gx_1'=4,'gx_2'=2,'gy'=16] {'gx_0','gx_1','gx_2'}, dimensions={0} | all-to-all | bytes 262144 | tf_op jit(solution)/shard_map/all_to_all | solution.py:380
  54.9 0.0 copy-done.5
  54.9 0.0 copy-done.6
  54.9 0.0 copy-done.7
  54.9 1.6 %shard_map.135 = (f32[32,8,256]{2,1,0:T(8,128)S(1)}, f32[2,32,256]{2,1,0:T(8,128)S(1)}) custom-call(s32[1]{0:T(128)S(6)} %copy.18.ids, f32[8,128]{1,0:T(8,128)S(1)} %get-tuple-element.19.count, bf16[32,16,128]{2,1,0:T(8,128)(2,1)S(1)} %all_to_all.26.recv, f32[8,128]{1,0:T(8,128)S(1)} %get-tuple-element.22.sides, f32[2,32,256]{2,1,0:T(8,128)S(1)} %copy-done, ...), custom_call_target="tpu_custom_call" | custom-call | flops 1000000 | bytes 1048576 | tf_op jit(solution)/shard_map/pallas_call | solution.py:419
  56.5 12.5 %all_to_all.27.recv = f32[32,8,256]{2,1,0:T(8,128)S(1)} all-to-all(f32[32,8,256]{2,1,0:T(8,128)S(1)} %get-tuple-element.23), channel_id=1, replica_groups=mesh['gx_0'=4,'gx_1'=4,'gx_2'=2,'gy'=16] {'gx_0','gx_1','gx_2'}, dimensions={0} | all-to-all | bytes 524288 | tf_op jit(solution)/shard_map/all_to_all | solution.py:380
  69.1 0.0 copy-start.3
  69.1 0.2 shard_map.136
  69.3 0.0 copy-start.4
  69.3 13.8 %all_to_all.28.recv = f32[16,2,128]{2,1,0:T(2,128)S(1)} all-to-all(f32[16,2,128]{2,1,0:T(2,128)S(1)} %shard_map.136), channel_id=1, replica_groups=mesh['gx_0'=4,'gx_1'=4,'gx_2'=2,'gy'=16] {'gy'}, dimensions={0} | all-to-all | bytes 32768 | tf_op jit(solution)/shard_map/all_to_all | solution.py:380
  83.1 0.0 copy-done.3
  83.1 0.0 copy-done.4
  83.1 0.8 shard_map.137
  (1 shorter events, 0.0 us)
Async XLA Ops:
  1.3 0.8 %copy-start = (f32[2,32,256]{2,1,0:T(8,128)S(1)}, f32[2,32,256]{2,1,0:T(8,128)}, u32[]{:S(2)}) copy-start(f32[2,32,256]{2,1,0:T(8,128)} %disp.7) | copy-start | bytes 196612
  1.3 0.8 copy-start.1
  1.3 0.8 copy-start.2
  42.1 12.8 %copy-start.5 = (s32[1,1024]{1,0:T(1,128)S(1)}, s32[1,1024]{1,0:T(1,128)}, u32[]{:S(2)}) copy-start(s32[1,1024]{1,0:T(1,128)} %pair_node.1) | copy-start | bytes 12292
  42.1 12.8 %copy-start.6 = (s32[1,1024]{1,0:T(1,128)S(1)}, s32[1,1024]{1,0:T(1,128)}, u32[]{:S(2)}) copy-start(s32[1,1024]{1,0:T(1,128)} %pair_segment.1) | copy-start | bytes 12292
  42.1 12.8 %copy-start.7 = (s32[1,1024]{1,0:T(1,128)S(1)}, s32[1,1024]{1,0:T(1,128)}, u32[]{:S(2)}) copy-start(s32[1,1024]{1,0:T(1,128)} %pair_side.1) | copy-start | bytes 12292
  69.1 14.0 %copy-start.3 = (f32[2,32,256]{2,1,0:T(8,128)S(1)}, f32[2,32,256]{2,1,0:T(8,128)}, u32[]{:S(2)}) copy-start(f32[2,32,256]{2,1,0:T(8,128)} %vel.1) | copy-start | bytes 196612
  69.3 13.8 %copy-start.4 = (f32[32,256]{1,0:T(8,128)S(1)}, f32[32,256]{1,0:T(8,128)}, u32[]{:S(2)}) copy-start(f32[32,256]{1,0:T(8,128)} %mass.7) | copy-start | bytes 98308

commit v6 on v5

--- a/solution.py
+++ b/solution.py
@@ -52,9 +52,16 @@
     return jnp.full((8, 128), count[0].astype(f32))
 
 
-def pick_kernel(owner, count, recv, chunk, tile):
-    chunk[...] = recv[owner[0] // NGY]
+def tile_kernel(owner, count, tile, at):
     tile[...] = count_tile(count)
+    at[...] = jnp.full((8, 128), owner[0] // NGY)
+
+
+def pick_kernel(at, recv, chunk):
+    picked = jnp.zeros((4, 4, 128), f32)
+    for s in range(NGX):
+        picked = jnp.where((at[0:4] == s)[None], recv[s].astype(f32), picked)
+    chunk[...] = picked.astype(bf16)
 
 
 def idle_kernel(count, chunk, tile):
@@ -385,7 +392,9 @@
     out = [((4, 4, 128), bf16), ((8, 128), f32)]
 
     def send(tiles, owner, count):
-        return tuple(call(pick_kernel, out, "ssv")(owner, count, exchange(tiles, GX)))
+        recv = exchange(tiles, GX)
+        tile, at = call(tile_kernel, [out[1], ((8, 128), jnp.int32)], "ss", flops=100_000_000)(owner, count)
+        return call(pick_kernel, out[:1], "vv")(at, recv)[0], tile
 
     def idle(tiles, owner, count):
         return tuple(call(idle_kernel, out, "s")(count))

time: 84.7 us -> 81.9 us (0.967); the launches traced: 83.9 us -> 83.5 us
  no operation moved by 1% of the time
where the time goes in v6:
time: 81.9 us; the launch traced here: 83.5 us
  blocking collectives  78.5 us (96%)
  Pallas kernels  3.39 us (4%)
  between operations  1.38 us (2%)
    all_to_all x4, blocking collectives, exchange(): return lax.all_to_all(value, axes, 0, 0, tiled=True)  78.5 us
    pallas_call x1, Pallas kernels, stages(): call(contact_kernel, [((NGX, 8, 256), f32), ((2, ROWS, COLS), f32)], 'svv...  1.65 us

profile of v6, /device:TPU:1, one launch (start us, length us, event | category | flops | bytes accessed | tf_op | source)
XLA Modules:
  0.0 83.5 jit_solution(17264874243870242845)
XLA Ops:
  1.3 0.0 copy-start
  1.3 0.0 copy-start.1
  1.3 0.0 copy-start.2
  1.3 0.7 conditional.1
  1.3 0.7 branch_0_fun.1
  2.0 0.1 copy-done
  2.1 0.0 copy-done.1
  2.1 0.0 copy-done.2
  2.1 0.1 shard_map.133
  2.2 39.4 %all_to_all.24.recv = bf16[16,3,4,128]{3,2,1,0:T(4,128)(2,1)S(1)} all-to-all(bf16[16,3,4,128]{3,2,1,0:T(4,128)(2,1)S(1)} %shard_map.133), channel_id=1, replica_groups=mesh['gx_0'=4,'gx_1'=4,'gx_2'=2,'gy'=16] {'gy'}, dimensions={0} | all-to-all | bytes 98304 | tf_op jit(solution)/shard_map/all_to_all | solution.py:387
  41.7 0.0 copy-start.5
  41.7 0.0 copy-start.6
  41.7 0.0 copy-start.7
  41.7 12.8 %all_to_all.25.recv = bf16[32,16,128]{2,1,0:T(8,128)(2,1)S(1)} all-to-all(bf16[32,16,128]{2,1,0:T(8,128)(2,1)S(1)} %get-tuple-element.23), channel_id=1, replica_groups=mesh['gx_0'=4,'gx_1'=4,'gx_2'=2,'gy'=16] {'gx_0','gx_1','gx_2'}, dimensions={0} | all-to-all | bytes 262144 | tf_op jit(solution)/shard_map/all_to_all | solution.py:387
  54.5 0.0 copy-done.5
  54.5 0.0 copy-done.6
  54.5 0.0 copy-done.7
  54.5 1.6 %shard_map.135 = (f32[32,8,256]{2,1,0:T(8,128)S(1)}, f32[2,32,256]{2,1,0:T(8,128)S(1)}) custom-call(s32[1]{0:T(128)S(6)} %copy.18.ids, f32[8,128]{1,0:T(8,128)S(1)} %get-tuple-element.21.count, bf16[32,16,128]{2,1,0:T(8,128)(2,1)S(1)} %all_to_all.25.recv, f32[8,128]{1,0:T(8,128)S(1)} %get-tuple-element.24.sides, f32[2,32,256]{2,1,0:T(8,128)S(1)} %copy-done, ...), custom_call_target="tpu_custom_call" | custom-call | flops 1000000 | bytes 1048576 | tf_op jit(solution)/shard_map/pallas_call | solution.py:428
  56.2 12.5 %all_to_all.26.recv = f32[32,8,256]{2,1,0:T(8,128)S(1)} all-to-all(f32[32,8,256]{2,1,0:T(8,128)S(1)} %get-tuple-element.25), channel_id=1, replica_groups=mesh['gx_0'=4,'gx_1'=4,'gx_2'=2,'gy'=16] {'gx_0','gx_1','gx_2'}, dimensions={0} | all-to-all | bytes 524288 | tf_op jit(solution)/shard_map/all_to_all | solution.py:387
  68.7 0.0 copy-start.3
  68.7 0.2 shard_map.136
  68.9 0.0 copy-start.4
  68.9 13.8 %all_to_all.27.recv = f32[16,2,128]{2,1,0:T(2,128)S(1)} all-to-all(f32[16,2,128]{2,1,0:T(2,128)S(1)} %shard_map.136), channel_id=1, replica_groups=mesh['gx_0'=4,'gx_1'=4,'gx_2'=2,'gy'=16] {'gy'}, dimensions={0} | all-to-all | bytes 32768 | tf_op jit(solution)/shard_map/all_to_all | solution.py:387
  82.7 0.0 copy-done.3
  82.7 0.0 copy-done.4
  82.7 0.8 shard_map.137
  (1 shorter events, 0.0 us)
Async XLA Ops:
  1.3 0.8 %copy-start = (f32[2,32,256]{2,1,0:T(8,128)S(1)}, f32[2,32,256]{2,1,0:T(8,128)}, u32[]{:S(2)}) copy-start(f32[2,32,256]{2,1,0:T(8,128)} %disp.7) | copy-start | bytes 196612
  1.3 0.8 copy-start.1
  1.3 0.8 copy-start.2
  41.7 12.8 %copy-start.5 = (s32[1,1024]{1,0:T(1,128)S(1)}, s32[1,1024]{1,0:T(1,128)}, u32[]{:S(2)}) copy-start(s32[1,1024]{1,0:T(1,128)} %pair_node.1) | copy-start | bytes 12292
  41.7 12.8 %copy-start.6 = (s32[1,1024]{1,0:T(1,128)S(1)}, s32[1,1024]{1,0:T(1,128)}, u32[]{:S(2)}) copy-start(s32[1,1024]{1,0:T(1,128)} %pair_segment.1) | copy-start | bytes 12292
  41.7 12.8 %copy-start.7 = (s32[1,1024]{1,0:T(1,128)S(1)}, s32[1,1024]{1,0:T(1,128)}, u32[]{:S(2)}) copy-start(s32[1,1024]{1,0:T(1,128)} %pair_side.1) | copy-start | bytes 12292
  68.7 14.0 %copy-start.3 = (f32[2,32,256]{2,1,0:T(8,128)S(1)}, f32[2,32,256]{2,1,0:T(8,128)}, u32[]{:S(2)}) copy-start(f32[2,32,256]{2,1,0:T(8,128)} %vel.1) | copy-start | bytes 196612
  68.9 13.8 %copy-start.4 = (f32[32,256]{1,0:T(8,128)S(1)}, f32[32,256]{1,0:T(8,128)}, u32[]{:S(2)}) copy-start(f32[32,256]{1,0:T(8,128)} %mass.7) | copy-start | bytes 98308

commit v7 on v6

--- a/solution.py
+++ b/solution.py
@@ -275,9 +275,11 @@
     lanes = one_hot(256, ends & 255)
     piece, line = ends >> 9, (ends >> 8) & 1
     looked = jnp.dot(coords[...], lanes, preferred_element_type=f32)
-    found = jnp.zeros((8, 2 * PAIRS), f32)
-    for s in range(NGX // 2):
-        found = found + jnp.where((piece >> 1) == s, looked[8 * s : 8 * s + 8], 0.0)
+    level = [looked[8 * s : 8 * s + 8] for s in range(NGX // 2)]
+    for bit in range(1, 5):
+        upper = ((piece >> bit) & 1) == 1
+        level = [jnp.where(upper, high, low) for low, high in zip(level[0::2], level[1::2])]
+    found = level[0]
     row = iota((8, 2 * PAIRS), 0)
     at = (piece & 1) * 4 + line
     end_x = jnp.sum(jnp.where(row == at, found, 0.0), axis=0, keepdims=True)

time: 81.9 us -> 82.4 us (level); the launches traced: 83.5 us -> 82 us
  blocking collectives: 78.5 us -> 77.2 us
    all_to_all x4, blocking collectives: 78.5 us -> 77.2 us  [exchange(): return lax.all_to_all(value, axes, 0, 0, tiled=True)]
where the time goes in v7:
time: 82.4 us; the launch traced here: 82 us
  blocking collectives  77.2 us (94%)
  Pallas kernels  3.26 us (4%)
  between operations  1.38 us (2%)
    all_to_all x4, blocking collectives, exchange(): return lax.all_to_all(value, axes, 0, 0, tiled=True)  77.2 us

profile of v7, /device:TPU:1, one launch (start us, length us, event | category | flops | bytes accessed | tf_op | source)
XLA Modules:
  0.0 82.0 jit_solution(12363519740660468990)
XLA Ops:
  1.3 0.0 copy-start
  1.3 0.0 copy-start.1
  1.3 0.0 copy-start.2
  1.3 0.7 conditional.1
  1.3 0.7 branch_0_fun.1
  2.0 0.1 copy-done
  2.1 0.0 copy-done.1
  2.1 0.0 copy-done.2
  2.1 0.1 shard_map.133
  2.2 38.1 %all_to_all.24.recv = bf16[16,3,4,128]{3,2,1,0:T(4,128)(2,1)S(1)} all-to-all(bf16[16,3,4,128]{3,2,1,0:T(4,128)(2,1)S(1)} %shard_map.133), channel_id=1, replica_groups=mesh['gx_0'=4,'gx_1'=4,'gx_2'=2,'gy'=16] {'gy'}, dimensions={0} | all-to-all | bytes 98304 | tf_op jit(solution)/shard_map/all_to_all | solution.py:389
  40.4 0.0 copy-start.5
  40.4 0.0 copy-start.6
  40.4 0.0 copy-start.7
  40.4 12.8 %all_to_all.25.recv = bf16[32,16,128]{2,1,0:T(8,128)(2,1)S(1)} all-to-all(bf16[32,16,128]{2,1,0:T(8,128)(2,1)S(1)} %get-tuple-element.23), channel_id=1, replica_groups=mesh['gx_0'=4,'gx_1'=4,'gx_2'=2,'gy'=16] {'gx_0','gx_1','gx_2'}, dimensions={0} | all-to-all | bytes 262144 | tf_op jit(solution)/shard_map/all_to_all | solution.py:389
  53.2 0.0 copy-done.5
  53.2 0.0 copy-done.6
  53.2 0.0 copy-done.7
  53.2 1.5 %shard_map.135 = (f32[32,8,256]{2,1,0:T(8,128)S(1)}, f32[2,32,256]{2,1,0:T(8,128)S(1)}) custom-call(s32[1]{0:T(128)S(6)} %copy.18.ids, f32[8,128]{1,0:T(8,128)S(1)} %get-tuple-element.21.count, bf16[32,16,128]{2,1,0:T(8,128)(2,1)S(1)} %all_to_all.25.recv, f32[8,128]{1,0:T(8,128)S(1)} %get-tuple-element.24.sides, f32[2,32,256]{2,1,0:T(8,128)S(1)} %copy-done, ...), custom_call_target="tpu_custom_call" | custom-call | flops 1000000 | bytes 1048576 | tf_op jit(solution)/shard_map/pallas_call | solution.py:430
  54.7 12.5 %all_to_all.26.recv = f32[32,8,256]{2,1,0:T(8,128)S(1)} all-to-all(f32[32,8,256]{2,1,0:T(8,128)S(1)} %get-tuple-element.25), channel_id=1, replica_groups=mesh['gx_0'=4,'gx_1'=4,'gx_2'=2,'gy'=16] {'gx_0','gx_1','gx_2'}, dimensions={0} | all-to-all | bytes 524288 | tf_op jit(solution)/shard_map/all_to_all | solution.py:389
  67.3 0.0 copy-start.3
  67.3 0.2 shard_map.136
  67.4 0.0 copy-start.4
  67.5 13.8 %all_to_all.27.recv = f32[16,2,128]{2,1,0:T(2,128)S(1)} all-to-all(f32[16,2,128]{2,1,0:T(2,128)S(1)} %shard_map.136), channel_id=1, replica_groups=mesh['gx_0'=4,'gx_1'=4,'gx_2'=2,'gy'=16] {'gy'}, dimensions={0} | all-to-all | bytes 32768 | tf_op jit(solution)/shard_map/all_to_all | solution.py:389
  81.3 0.0 copy-done.3
  81.3 0.0 copy-done.4
  81.3 0.8 shard_map.137
  (1 shorter events, 0.0 us)
Async XLA Ops:
  1.3 0.8 %copy-start = (f32[2,32,256]{2,1,0:T(8,128)S(1)}, f32[2,32,256]{2,1,0:T(8,128)}, u32[]{:S(2)}) copy-start(f32[2,32,256]{2,1,0:T(8,128)} %disp.7) | copy-start | bytes 196612
  1.3 0.8 %copy-start.1 = (f32[32,256]{1,0:T(8,128)S(1)}, f32[32,256]{1,0:T(8,128)}, u32[]{:S(2)}) copy-start(f32[32,256]{1,0:T(8,128)} %energy.5) | copy-start | bytes 98308
  1.3 0.8 %copy-start.2 = (f32[32,256]{1,0:T(8,128)S(1)}, f32[32,256]{1,0:T(8,128)}, u32[]{:S(2)}) copy-start(f32[32,256]{1,0:T(8,128)} %mass.6) | copy-start | bytes 98308
  40.4 12.8 %copy-start.5 = (s32[1,1024]{1,0:T(1,128)S(1)}, s32[1,1024]{1,0:T(1,128)}, u32[]{:S(2)}) copy-start(s32[1,1024]{1,0:T(1,128)} %pair_node.1) | copy-start | bytes 12292
  40.4 12.8 %copy-start.6 = (s32[1,1024]{1,0:T(1,128)S(1)}, s32[1,1024]{1,0:T(1,128)}, u32[]{:S(2)}) copy-start(s32[1,1024]{1,0:T(1,128)} %pair_segment.1) | copy-start | bytes 12292
  40.4 12.8 %copy-start.7 = (s32[1,1024]{1,0:T(1,128)S(1)}, s32[1,1024]{1,0:T(1,128)}, u32[]{:S(2)}) copy-start(s32[1,1024]{1,0:T(1,128)} %pair_side.1) | copy-start | bytes 12292
  67.3 14.0 %copy-start.3 = (f32[2,32,256]{2,1,0:T(8,128)S(1)}, f32[2,32,256]{2,1,0:T(8,128)}, u32[]{:S(2)}) copy-start(f32[2,32,256]{2,1,0:T(8,128)} %vel.1) | copy-start | bytes 196612
  67.4 13.8 %copy-start.4 = (f32[32,256]{1,0:T(8,128)S(1)}, f32[32,256]{1,0:T(8,128)}, u32[]{:S(2)}) copy-start(f32[32,256]{1,0:T(8,128)} %mass.7) | copy-start | bytes 98308

commit v8 on v7

--- a/solution.py
+++ b/solution.py
@@ -234,10 +234,15 @@
     lanes, mask = node_place(pair_node[...])
     seen = jnp.dot(nodes[...], lanes, preferred_element_type=f32)
     seen = (seen[256:384] + seen[128:256]) + seen[0:128]
-    found = [
-        jnp.sum(jnp.where(mask, seen[64 * c : 64 * c + 64], 0.0), axis=0, keepdims=True)
-        for c in range(2)
-    ]
+    row = ((pair_node[...] >> 7) & 1) * 32 + (pair_node[...] >> 8)
+    found = []
+    for c in range(2):
+        level = [seen[64 * c + 8 * g : 64 * c + 8 * g + 8] for g in range(8)]
+        for bit in range(3, 6):
+            upper = ((row >> bit) & 1) == 1
+            level = [jnp.where(upper, high, low) for low, high in zip(level[0::2], level[1::2])]
+        one = jnp.where(iota((8, PAIRS), 0) == (row & 7), level[0], 0.0)
+        found.append(jnp.sum(one, axis=0, keepdims=True))
     return found, lanes, mask
 
 

time: 82.4 us -> 86.1 us (1.045)
  blocking collectives: 77.2 us -> 80.7 us
    all_to_all x4, blocking collectives: 77.2 us -> 80.7 us  [exchange(): return lax.all_to_all(value, axes, 0, 0, tiled=True)]
where the time goes in v8:
time: 86.1 us; the launch traced here: 85.4 us
  blocking collectives  80.7 us (94%)
  Pallas kernels  3.23 us (4%)
  between operations  1.38 us (2%)
    all_to_all x4, blocking collectives, exchange(): return lax.all_to_all(value, axes, 0, 0, tiled=True)  80.7 us

profile of v8, /device:TPU:1, one launch (start us, length us, event | category | flops | bytes accessed | tf_op | source)
XLA Modules:
  0.0 85.4 jit_solution(1326287760843707065)
XLA Ops:
  1.3 0.0 copy-start
  1.3 0.0 copy-start.1
  1.3 0.0 copy-start.2
  1.3 0.7 conditional.1
  1.3 0.7 branch_0_fun.1
  2.0 0.1 copy-done
  2.1 0.0 copy-done.1
  2.1 0.0 copy-done.2
  2.1 0.1 shard_map.133
  2.2 41.5 %all_to_all.24.recv = bf16[16,3,4,128]{3,2,1,0:T(4,128)(2,1)S(1)} all-to-all(bf16[16,3,4,128]{3,2,1,0:T(4,128)(2,1)S(1)} %shard_map.133), channel_id=1, replica_groups=mesh['gx_0'=4,'gx_1'=4,'gx_2'=2,'gy'=16] {'gy'}, dimensions={0} | all-to-all | bytes 98304 | tf_op jit(solution)/shard_map/all_to_all | solution.py:394
  43.8 0.0 copy-start.5
  43.8 0.0 copy-start.6
  43.8 0.0 copy-start.7
  43.8 12.8 %all_to_all.25.recv = bf16[32,16,128]{2,1,0:T(8,128)(2,1)S(1)} all-to-all(bf16[32,16,128]{2,1,0:T(8,128)(2,1)S(1)} %get-tuple-element.23), channel_id=1, replica_groups=mesh['gx_0'=4,'gx_1'=4,'gx_2'=2,'gy'=16] {'gx_0','gx_1','gx_2'}, dimensions={0} | all-to-all | bytes 262144 | tf_op jit(solution)/shard_map/all_to_all | solution.py:394
  56.6 0.0 copy-done.5
  56.6 0.0 copy-done.6
  56.6 0.0 copy-done.7
  56.6 1.5 %shard_map.135 = (f32[32,8,256]{2,1,0:T(8,128)S(1)}, f32[2,32,256]{2,1,0:T(8,128)S(1)}) custom-call(s32[1]{0:T(128)S(6)} %copy.18.ids, f32[8,128]{1,0:T(8,128)S(1)} %get-tuple-element.21.count, bf16[32,16,128]{2,1,0:T(8,128)(2,1)S(1)} %all_to_all.25.recv, f32[8,128]{1,0:T(8,128)S(1)} %get-tuple-element.24.sides, f32[2,32,256]{2,1,0:T(8,128)S(1)} %copy-done, ...), custom_call_target="tpu_custom_call" | custom-call | flops 1000000 | bytes 1048576 | tf_op jit(solution)/shard_map/pallas_call | solution.py:435
  58.1 12.5 %all_to_all.26.recv = f32[32,8,256]{2,1,0:T(8,128)S(1)} all-to-all(f32[32,8,256]{2,1,0:T(8,128)S(1)} %get-tuple-element.25), channel_id=1, replica_groups=mesh['gx_0'=4,'gx_1'=4,'gx_2'=2,'gy'=16] {'gx_0','gx_1','gx_2'}, dimensions={0} | all-to-all | bytes 524288 | tf_op jit(solution)/shard_map/all_to_all | solution.py:394
  70.7 0.0 copy-start.3
  70.7 0.2 shard_map.136
  70.8 0.0 copy-start.4
  70.9 13.8 %all_to_all.27.recv = f32[16,2,128]{2,1,0:T(2,128)S(1)} all-to-all(f32[16,2,128]{2,1,0:T(2,128)S(1)} %shard_map.136), channel_id=1, replica_groups=mesh['gx_0'=4,'gx_1'=4,'gx_2'=2,'gy'=16] {'gy'}, dimensions={0} | all-to-all | bytes 32768 | tf_op jit(solution)/shard_map/all_to_all | solution.py:394
  84.7 0.0 copy-done.3
  84.7 0.0 copy-done.4
  84.7 0.8 shard_map.137
  (1 shorter events, 0.0 us)
Async XLA Ops:
  1.3 0.8 copy-start
  1.3 0.8 copy-start.1
  1.3 0.8 copy-start.2
  43.8 12.8 %copy-start.5 = (s32[1,1024]{1,0:T(1,128)S(1)}, s32[1,1024]{1,0:T(1,128)}, u32[]{:S(2)}) copy-start(s32[1,1024]{1,0:T(1,128)} %pair_node.1) | copy-start | bytes 12292
  43.8 12.8 %copy-start.6 = (s32[1,1024]{1,0:T(1,128)S(1)}, s32[1,1024]{1,0:T(1,128)}, u32[]{:S(2)}) copy-start(s32[1,1024]{1,0:T(1,128)} %pair_segment.1) | copy-start | bytes 12292
  43.8 12.8 %copy-start.7 = (s32[1,1024]{1,0:T(1,128)S(1)}, s32[1,1024]{1,0:T(1,128)}, u32[]{:S(2)}) copy-start(s32[1,1024]{1,0:T(1,128)} %pair_side.1) | copy-start | bytes 12292
  70.7 14.0 %copy-start.3 = (f32[2,32,256]{2,1,0:T(8,128)S(1)}, f32[2,32,256]{2,1,0:T(8,128)}, u32[]{:S(2)}) copy-start(f32[2,32,256]{2,1,0:T(8,128)} %vel.1) | copy-start | bytes 196612
  70.8 13.8 %copy-start.4 = (f32[32,256]{1,0:T(8,128)S(1)}, f32[32,256]{1,0:T(8,128)}, u32[]{:S(2)}) copy-start(f32[32,256]{1,0:T(8,128)} %mass.7) | copy-start | bytes 98308
